TPU v7x, 768 devices: a whole 4x8x12 slice. The times are simulated.
768 devices in a mesh: grp: 24 (over y_lo, z), tp: 32 (over x, y_hi, core).
Axes of the slice: x: 4, y: 8 (y_hi: 4, y_lo: 2; y = y_hi * 2 + y_lo), z: 12, core: 2. Of those that a mesh axis runs over, the one named last changes fastest.
Arguments:
- hidden: bfloat16 [6144, 8192], P('grp'), may hold values from -30 to 30
- proj_weight: bfloat16 [8192, 8192], P(None, 'tp'), may hold values from -0.32040776 to 0.32040776
- proj_bias: float32 [8192], P('tp'), may hold values from -3 to 3
- tile_pos: int32 [768], replicated, may hold values from 0 to 2303, as said below
- text_embed: bfloat16 [18432, 8192], P('grp', 'tp'), may hold values from -76 to 76
- norm_gain: float32 [8192], P('tp'), may hold values from 0.25 to 1.75
- d_normed: bfloat16 [18432, 8192], P('grp', 'tp'), may hold values from -6 to 6
Outputs:
- normed: bfloat16 [18432, 8192], P('grp', 'tp')
- d_text: bfloat16 [18432, 8192], P('grp', 'tp')
- d_hidden: bfloat16 [6144, 8192], P('grp', 'tp')
Inputs may be any that keep to these rules, and one draw needn't show every extreme that they name: `tile_pos`: all positions are distinct. Of the tiles k * 32 to (k + 1) * 32 - 1, at most 2 lie in the 96 tile positions of one index of grp, and in every draw each such block has exactly 2 tiles in some index of grp.
All inputs are finite; a program needn't handle non-finite values.
Results may differ from a plain program's by a relative error of at most 0.015.
Values may be sent and summed in bfloat16 or wider, within the bound.
No kernel may reach another device: no remote copies, remote signals or barrier semaphores. Data moves between devices by JAX's collectives and lax.ppermute only.
A program may use at most 64 MiB of HBM per device.

v0:
```python
import jax
import jax.numpy as jnp
from jax import lax
from jax.sharding import PartitionSpec as P

TILE = 8


epsilon = 1e-05


def copy_for_each(value, axis):
    copies = jnp.broadcast_to(value, (lax.axis_size(axis), *value.shape))
    return lax.all_to_all(copies, axis, split_axis=0, concat_axis=0, tiled=True)


def over_copies(value, axis):
    everything = copy_for_each(value, axis)
    return jnp.sum(everything, axis=0)


def packed_total(arrays, axis):
    ends = [0]
    for a in arrays:
        ends.append(ends[-1] + a.size)
    running = over_copies(jnp.concatenate([a.ravel() for a in arrays]), axis)
    return tuple((running[b:e].reshape(a.shape) for a, b, e in zip(arrays, ends, ends[1:])))


def gelu_slope(values):
    normal_cdf = 0.5 * (1.0 + lax.erf(values * 0.7071067811865476))
    density = jnp.exp(-0.5 * values * values) * 0.3989422804014327
    return normal_cdf + values * density


def match_table(wanted, choices_count):
    return wanted[None, :] == jnp.arange(choices_count, dtype=jnp.int32)[:, None]


def on_device(hidden, proj_weight, proj_bias, tile_pos, text_embed, norm_gain, d_normed):
    rows_dev = hidden.shape[0]
    model_width = hidden.shape[1]
    local_cols = proj_weight.shape[1]
    tok_dev = text_embed.shape[0]
    groups = lax.axis_size("grp")
    group_index = lax.axis_index("grp")
    lane_index = lax.axis_index("tp")
    tiles_dev = rows_dev // TILE
    spread = tok_dev // TILE
    total_tiles = tiles_dev * groups
    tile_width = TILE * local_cols
    capacity = max(2, (tiles_dev + groups - 1) // groups)
    activated = jax.nn.gelu(hidden.astype(jnp.float32), approximate=False).astype(jnp.bfloat16)
    image_rows = jnp.dot(activated, proj_weight, preferred_element_type=jnp.float32) + proj_bias
    tile_rows = image_rows.astype(jnp.bfloat16).reshape(tiles_dev, tile_width)
    target = tile_pos // spread
    local_pos = tile_pos - group_index * spread
    hits = match_table(local_pos, spread)
    is_image = jnp.any(hits, axis=1)
    place = hits.astype(jnp.bfloat16)
    tile_index = jnp.arange(total_tiles, dtype=jnp.int32)
    source = tile_index // tiles_dev
    earlier = (
        (source[:, None] == source[None, :])
        & (target[:, None] == target[None, :])
        & (tile_index[None, :] < tile_index[:, None])
    )
    standing = jnp.sum(earlier.astype(jnp.int32), axis=1)
    send_slot = lax.dynamic_slice_in_dim(
        target * capacity + standing, group_index * tiles_dev, tiles_dev, 0
    )
    sender = match_table(send_slot, groups * capacity).astype(jnp.bfloat16)
    outgoing = jnp.dot(sender, tile_rows, preferred_element_type=jnp.float32).astype(jnp.bfloat16)
    incoming = lax.all_to_all(outgoing, "grp", split_axis=0, concat_axis=0, tiled=True)
    arrival = match_table(source * capacity + standing, groups * capacity).astype(jnp.bfloat16)
    receiver = lax.dot_general(
        place, arrival, (((1,), (1,)), ((), ())), preferred_element_type=jnp.float32
    ).astype(jnp.bfloat16)
    placed = jnp.dot(receiver, incoming, preferred_element_type=jnp.float32)
    base_rows = text_embed.reshape(spread, tile_width)
    merged = jnp.where(is_image[:, None], placed.astype(jnp.bfloat16), base_rows).reshape(
        tok_dev, local_cols
    )
    wide_merged = merged.astype(jnp.float32)
    grad_in = d_normed.astype(jnp.float32) * norm_gain
    squares, crosses = packed_total(
        (jnp.sum(wide_merged * wide_merged, axis=1), jnp.sum(grad_in * wide_merged, axis=1)), "tp"
    )
    inverse = lax.rsqrt(squares / model_width + epsilon)[:, None]
    cross_mean = (crosses / model_width)[:, None]
    normed = (wide_merged * inverse * norm_gain).astype(jnp.bfloat16)
    d_merged = inverse * (grad_in - wide_merged * inverse * inverse * cross_mean)
    d_tiles = d_merged.reshape(spread, tile_width)
    d_text = (
        jnp.where(is_image[:, None], 0.0, d_tiles).astype(jnp.bfloat16).reshape(tok_dev, local_cols)
    )
    d_image_tiles = d_tiles.astype(jnp.bfloat16)
    back_out = lax.dot_general(
        receiver, d_image_tiles, (((0,), (0,)), ((), ())), preferred_element_type=jnp.float32
    ).astype(jnp.bfloat16)
    back_in = lax.all_to_all(back_out, "grp", split_axis=0, concat_axis=0, tiled=True)
    returned = lax.dot_general(
        sender, back_in, (((0,), (0,)), ((), ())), preferred_element_type=jnp.float32
    )
    d_image = returned.astype(jnp.bfloat16).reshape(rows_dev, local_cols)
    partial_grads = lax.dot_general(
        d_image, proj_weight, (((1,), (1,)), ((), ())), preferred_element_type=jnp.float32
    )
    d_act = lax.psum_scatter(
        partial_grads.astype(jnp.bfloat16), "tp", scatter_dimension=1, tiled=True
    ).astype(jnp.float32)
    own_hidden = lax.dynamic_slice_in_dim(hidden, lane_index * local_cols, local_cols, 1).astype(
        jnp.float32
    )
    d_hidden = (d_act * gelu_slope(own_hidden)).astype(jnp.bfloat16)
    return (normed, d_text, d_hidden)


def solution(mesh):
    in_specs = (
        P("grp", None),
        P(None, "tp"),
        P("tp"),
        P(),
        P("grp", "tp"),
        P("tp"),
        P("grp", "tp"),
    )
    out_specs = (P("grp", "tp"), P("grp", "tp"), P("grp", "tp"))
    return jax.shard_map(
        on_device, mesh=mesh, in_specs=in_specs, out_specs=out_specs, check_vma=False
    )
```

profile of v0, /device:TPU:64, one launch (start us, length us, event | category | flops | bytes accessed | tf_op | source)
XLA Modules:
  0.0 222.2 jit_solution(8076537397332618818)
XLA Ops:
  7.2 0.7 add_select_fusion
  7.9 20.2 %fusion.39 = bf16[256,256]{1,0:T(8,128)(2,1)S(1)} fusion(bf16[8192,256]{1,0:T(8,128)(2,1)} %param.8, bf16[256,8192]{1,0:T(8,128)(2,1)} %param.7, f32[256]{0:T(256)} %param.9), kind=kOutput, calls=%fused_computation.46 | convolution fusion | flops 1212284928 | bytes 8520704 | tf_op jit(solution)/shard_map/dot_general | solution.py:54
  28.2 0.5 convert_reduce_fusion
  28.7 0.1 dynamic_slice.6
  28.8 0.2 convolution_convert_fusion.3
  29.0 0.8 all_to_all.20
  29.8 15.9 %all-to-all-start = ((bf16[24,2,2048]{2,1,0:T(2,128)(2,1)}), bf16[24,2,2048]{2,1,0:T(2,128)(2,1)S(1)}, u32[]{:S(2)}, u32[]{:S(2)}) async-start(bf16[24,2,2048]{2,1,0:T(2,128)(2,1)} %all_to_all.20), calls=%async_computation | async-start | bytes 393216 | tf_op jit(solution)/shard_map/all_to_all | solution.py:74
  45.7 0.2 reshape.72
  45.9 0.1 fusion.42
  46.0 0.2 convolution_convert_fusion.5
  46.2 11.7 %all-to-all-done = bf16[24,2,2048]{2,1,0:T(2,128)(2,1)S(1)} async-done(((bf16[24,2,2048]{2,1,0:T(2,128)(2,1)}), bf16[24,2,2048]{2,1,0:T(2,128)(2,1)S(1)}, u32[]{:S(2)}, u32[]{:S(2)}) %all-to-all-start) | async-done | bytes 196640 | tf_op jit(solution)/shard_map/all_to_all | solution.py:74
  57.9 0.1 all_to_all.22
  57.9 0.3 fusion.35
  58.2 0.1 reshape.74
  58.4 0.3 multiply_reduce_fusion.1
  58.7 0.8 broadcast_in_dim.23
  59.5 9.1 %all-to-all-start.1 = ((f32[32,1,1536]{2,1,0:T(1,128)}), f32[32,1,1536]{2,1,0:T(1,128)S(1)}, u32[]{:S(2)}, u32[]{:S(2)}) async-start(f32[32,1,1536]{2,1,0:T(1,128)} %broadcast_in_dim.23), calls=%async_computation.1 | async-start | bytes 393216 | tf_op jit(solution)/shard_map/all_to_all | solution.py:14
  68.6 0.1 broadcast_in_dim.24
  68.7 0.1 broadcast_in_dim.25
  68.8 12.3 %all-to-all-done.1 = f32[32,1,1536]{2,1,0:T(1,128)S(1)} async-done(((f32[32,1,1536]{2,1,0:T(1,128)}), f32[32,1,1536]{2,1,0:T(1,128)S(1)}, u32[]{:S(2)}, u32[]{:S(2)}) %all-to-all-start.1) | async-done | bytes 196640 | tf_op jit(solution)/shard_map/all_to_all | solution.py:14
  81.0 0.1 reduce_sum.39
  81.2 1.2 fusion.91
  82.4 0.2 convert_element_type.77
  82.6 0.2 convolution_convert_fusion.2
  82.8 0.1 all_to_all.24
  83.0 17.5 %all_to_all.30 = bf16[24,2,2048]{2,1,0:T(2,128)(2,1)S(1)} all-to-all(bf16[24,2,2048]{2,1,0:T(2,128)(2,1)S(1)} %all_to_all.24), channel_id=1, replica_groups=mesh['grp'=24,'tp'=32] {'grp'}, dimensions={0} | all-to-all | bytes 393216 | tf_op jit(solution)/shard_map/all_to_all | solution.py:101
  100.5 0.1 all_to_all.26
  100.5 0.2 convolution_convert_fusion.4
  100.8 0.1 reshape.73
  100.8 5.4 %convolution_convert_fusion = bf16[256,8192]{1,0:T(8,128)(2,1)} fusion(bf16[256,256]{1,0:T(8,128)(2,1)S(1)} %reshape.73, bf16[8192,256]{1,0:T(8,128)(2,1)} %param.8), kind=kOutput, calls=%fused_computation.3 | convolution fusion | flops 1075838976 | bytes 8519680 | tf_op jit(solution)/shard_map/dot_general | solution.py:106
  106.3 107.4 %reduce-scatter.2.cloned.1.call-done = bf16[256,256]{1,0:T(8,128)(2,1)} async-done(((bf16[256,8192]{1,0:T(8,128)(2,1)}), bf16[256,256]{1,0:T(8,128)(2,1)}) %reduce-scatter.2.cloned.1.call-update) | async-done | bytes 131088 | tf_op jit(solution)/shard_map/reduce_scatter | solution.py:109
  213.6 1.7 fusion.50
  (14 shorter events, 0.2 us)
Async XLA Ops:
  7.9 20.8 %copy-start.2 = (s32[768]{0:T(1024)S(1)}, s32[768]{0:T(1024)}, u32[]{:S(2)}) copy-start(s32[768]{0:T(1024)} %param.10) | copy-start | bytes 9220
  7.9 37.8 %copy-start.1 = (bf16[768,256]{1,0:T(8,128)(2,1)S(1)}, bf16[768,256]{1,0:T(8,128)(2,1)}, u32[]{:S(2)}) copy-start(bf16[768,256]{1,0:T(8,128)(2,1)} %param.11) | copy-start | bytes 1179652
  28.1 30.2 %copy-start = (bf16[768,256]{1,0:T(8,128)(2,1)S(1)}, bf16[768,256]{1,0:T(8,128)(2,1)}, u32[]{:S(2)}) copy-start(bf16[768,256]{1,0:T(8,128)(2,1)} %param.13) | copy-start | bytes 1179652
  28.1 30.2 %copy-start.3 = (f32[256]{0:T(256)S(1)}, f32[256]{0:T(256)}, u32[]{:S(2)}) copy-start(f32[256]{0:T(256)} %param.12) | copy-start | bytes 3076
  29.8 28.0 %all-to-all-start = ((bf16[24,2,2048]{2,1,0:T(2,128)(2,1)}), bf16[24,2,2048]{2,1,0:T(2,128)(2,1)S(1)}, u32[]{:S(2)}, u32[]{:S(2)}) async-start(bf16[24,2,2048]{2,1,0:T(2,128)(2,1)} %all_to_all.20), calls=%async_computation | async-start | bytes 393216 | tf_op jit(solution)/shard_map/all_to_all | solution.py:74
  59.5 21.6 %all-to-all-start.1 = ((f32[32,1,1536]{2,1,0:T(1,128)}), f32[32,1,1536]{2,1,0:T(1,128)S(1)}, u32[]{:S(2)}, u32[]{:S(2)}) async-start(f32[32,1,1536]{2,1,0:T(1,128)} %broadcast_in_dim.23), calls=%async_computation.1 | async-start | bytes 393216 | tf_op jit(solution)/shard_map/all_to_all | solution.py:14
  68.5 145.1 %reduce-scatter.2.cloned.1.call-start = ((), (), s32[]{:S(2)}) async-start(), calls=%async_computation.4 | async-start | bytes 4325376 | tf_op jit(solution)/shard_map/reduce_scatter | solution.py:109
Sparse Core Ops, SparseCore 0:
  106.4 107.2 reduce-scatter.1
where the time goes:
time: 223 us; the launch traced here: 222 us
  waiting for transfers between devices  131 us (59%)
  matrix products  26.7 us (12%)
  starting transfers between devices  24.9 us (11%)
  blocking collectives  17.5 us (8%)
  between operations  14.3 us (6%)
  other arithmetic  4.76 us (2%)
  local copies, waits for them, and re-layouts  2.79 us (1%)
    reduce_scatter x1, waiting for transfers between devices, on_device(): lax.psum_scatter(partial_grads.astype(jnp.bfloat16), 'tp', scatter_dimens...  107 us
    dot_general x1, matrix products, on_device(): jnp.dot(activated, proj_weight, preferred_element_type=jnp.float32)  20.2 us
    all_to_all x1, blocking collectives, on_device(): lax.all_to_all(back_out, 'grp', split_axis=0, concat_axis=0, tiled=True)  17.5 us
    all_to_all x1, starting transfers between devices, on_device(): lax.all_to_all(outgoing, 'grp', split_axis=0, concat_axis=0, tiled=True)  15.9 us
    all_to_all x1, waiting for transfers between devices, copy_for_each(): return lax.all_to_all(copies, axis, split_axis=0, concat_axis=0, tiled=True)  12.3 us
    all_to_all x1, waiting for transfers between devices, on_device(): lax.all_to_all(outgoing, 'grp', split_axis=0, concat_axis=0, tiled=True)  11.7 us
    all_to_all x1, starting transfers between devices, copy_for_each(): return lax.all_to_all(copies, axis, split_axis=0, concat_axis=0, tiled=True)  9.05 us
    dot_general x1, matrix products, on_device(): lax.dot_general(d_image, proj_weight, (((1,), (1,)), ((), ())), preferred...  5.41 us
  transfers between devices with their start and end apart: 3, of which 3 were waited for; matrix products, arithmetic and copies ran while one was open for 0% of the time, Pallas kernels for 0%

commit v1 on v0

v1 whole, which is shorter than its diff:
```python
import jax
import jax.numpy as jnp
from jax import lax
from jax.experimental import pallas as pl
from jax.experimental.pallas import tpu as pltpu
from jax.sharding import Mesh, PartitionSpec as P


TILE = 8
X, Y, C = 4, 4, 2
LANES = 128
GRANT = 16 << 20
LARGE_GRANT = 49 << 20

epsilon = 1e-05
bf16, f32 = jnp.bfloat16, jnp.float32


def gelu(values):
    return values * (0.5 * (1.0 + lax.erf(values * 0.7071067811865476)))


def gelu_slope(values):
    normal_cdf = 0.5 * (1.0 + lax.erf(values * 0.7071067811865476))
    density = jnp.exp(-0.5 * values * values) * 0.3989422804014327
    return normal_cdf + values * density


def match_table(wanted, choices_count):
    return wanted[None, :] == jnp.arange(choices_count, dtype=jnp.int32)[:, None]


def row_sums(image_rows, pair_rows, image_grad, pair_grad, text_embed, d_normed, norm_gain):
    rows, cols = image_rows.shape
    texts = text_embed.shape[0] // rows
    count = 2 + 2 * texts

    def kernel(image_r, pair_r, image_g, pair_g, text_r, d_r, gain_r, o_ref):
        lane = lax.broadcasted_iota(jnp.int32, (rows, LANES), 1)
        table = jnp.zeros((rows, LANES), f32)

        def put(table, index, values):
            return jnp.where(lane == index, jnp.sum(values, axis=1, keepdims=True), table)

        wide, pair = image_r[...].astype(f32), pair_r[...].astype(f32)
        table = put(table, 0, wide * wide + pair * pair)
        table = put(table, 1, image_g[...] * wide + pair_g[...] * pair)
        for i in range(texts):
            text = text_r[pl.ds(i * rows, rows), :].astype(f32)
            grad = d_r[pl.ds(i * rows, rows), :].astype(f32) * gain_r[...]
            table = put(table, 2 + i, text * text)
            table = put(table, 2 + texts + i, grad * text)
        flat = table.T[:count]
        o_ref[...] = jnp.broadcast_to(flat[None], (X * Y, count, rows))

    return pl.pallas_call(
        kernel,
        out_shape=jax.ShapeDtypeStruct((X * Y, count, rows), f32),
        compiler_params=pltpu.CompilerParams(vmem_limit_bytes=GRANT),
        cost_estimate=pl.CostEstimate(
            flops=8 * rows * cols * (texts + 2), bytes_accessed=4 * rows * cols * (texts + 3), transcendentals=0
        ),
    )(image_rows, pair_rows, image_grad, pair_grad, text_embed, d_normed, norm_gain)


def product(own_weight, pair_weight, sums, rows_pair, grads_pair, norm_gain, picks, core, width):
    features, cols = own_weight.shape[-2:]
    rows = rows_pair[0].shape[0]
    half = Y // 2
    groups, each = 4, 2
    steps = groups * each

    def kernel(pick, own_w, pair_w, sums_r, own_r, pair_r, own_g, pair_g, gain, *rest):
        normed, outs, own_d, pair_d = rest[0], rest[1:5], rest[5], rest[6]
        step = pl.program_id(0)

        @pl.when(step == 0)
        def _():
            total = jnp.sum(sums_r[...], axis=0)
            full = jnp.concatenate([total, jnp.zeros((LANES - total.shape[0], rows), f32)], axis=0)
            columns = full.T
            inverse = lax.rsqrt(columns[:, 0:1] / width + epsilon)
            cross_mean = columns[:, 1:2] / width

            def gradient(wide, grad):
                d_rows = inverse * (grad - wide * inverse * inverse * cross_mean)
                return d_rows.astype(bf16)

            wide = own_r[...].astype(f32)
            own_d[...] = gradient(wide, own_g[...])
            pair_d[...] = gradient(pair_r[...].astype(f32), pair_g[...])
            normed[...] = (wide * inverse * gain[...]).astype(bf16)

        def part(w, g):
            return lax.dot_general(
                w[...].reshape(half * features, cols),
                g[...],
                (((1,), (1,)), ((), ())),
                preferred_element_type=f32,
            )

        total = part(own_w, own_d) + part(pair_w, pair_d)
        total = total.astype(bf16).reshape(1, half, features, rows)
        for k, out in enumerate(outs):

            @pl.when(step // each == k)
            def _(out=out):
                out[...] = total

    def whole(*shape):
        return pl.BlockSpec(shape, lambda i, s: (0,) * len(shape))

    weight_spec = pl.BlockSpec(
        (None, half, None, features, cols), lambda i, s: (s[i], (i // each) % 2, s[steps], 0, 0)
    )

    def out_spec(k):
        return pl.BlockSpec(
            (1, half, features, rows), lambda i, s: (jnp.clip(i - each * k, 0, each - 1), 0, 0, 0)
        )

    return pl.pallas_call(
        kernel,
        grid_spec=pltpu.PrefetchScalarGridSpec(
            num_scalar_prefetch=1,
            grid=(steps,),
            in_specs=[weight_spec, weight_spec, whole(*sums.shape)]
            + [whole(rows, cols)] * 4
            + [whole(1, cols)],
            out_specs=[whole(rows, cols)] + [out_spec(k) for k in range(groups)],
            scratch_shapes=[pltpu.VMEM((rows, cols), bf16)] * 2,
        ),
        out_shape=[jax.ShapeDtypeStruct((rows, cols), bf16)]
        + [jax.ShapeDtypeStruct((each, half, features, rows), bf16)] * groups,
        compiler_params=pltpu.CompilerParams(vmem_limit_bytes=LARGE_GRANT),
        cost_estimate=pl.CostEstimate(
            flops=4 * steps * half * features * cols * rows,
            bytes_accessed=2 * steps * half * features * (2 * cols + rows),
            transcendentals=rows,
        ),
    )(jnp.stack([*picks, core]), own_weight, pair_weight, sums, *rows_pair, *grads_pair, norm_gain)


def combined(kept_a, got_a, last_a, kept_b, got_b, last_b):
    half, features, rows = last_a.shape

    def kernel(kept_a, got_a, last_a, kept_b, got_b, last_b, o_ref):
        for at, parts in ((0, (kept_a, got_a, last_a)), (half, (kept_b, got_b, last_b))):
            total = sum(part[...].astype(f32) for part in parts)
            o_ref[pl.ds(at, half)] = total.astype(bf16)

    second = pl.BlockSpec((None, half, features, rows), lambda i: (1, 0, 0, 0))
    whole = pl.BlockSpec((half, features, rows), lambda i: (0, 0, 0))
    return pl.pallas_call(
        kernel,
        grid=(1,),
        in_specs=[second, second, whole] * 2,
        out_specs=pl.BlockSpec((2 * half, features, rows), lambda i: (0, 0, 0)),
        out_shape=jax.ShapeDtypeStruct((2 * half, features, rows), bf16),
        compiler_params=pltpu.CompilerParams(vmem_limit_bytes=GRANT),
        cost_estimate=pl.CostEstimate(
            flops=4 * half * features * rows,
            bytes_accessed=16 * half * features * rows,
            transcendentals=0,
        ),
    )(kept_a, got_a, last_a, kept_b, got_b, last_b)


def swap_pair(value):
    return lax.ppermute(value, "core", [(0, 1), (1, 0)])


def swap_even(value):
    return lax.ppermute(value, "x", [(i, i ^ 1) for i in range(X)])


def swap_odd(value):
    return lax.ppermute(value, "x", [(i, 3 - i) for i in range(X)])


def swap_all(value, axis):
    return lax.all_to_all(value, axis, split_axis=0, concat_axis=0, tiled=True)


def on_device(hidden, proj_weight, proj_bias, tile_pos, text_embed, norm_gain, d_normed):
    rows_dev, model_width = hidden.shape
    local_cols = proj_weight.shape[1]
    tok_dev = text_embed.shape[0]
    groups = lax.axis_size("grp")
    group_index = lax.axis_index("grp")
    core = lax.axis_index("core")
    here = lax.axis_index("x")
    lane_index = (here * Y + lax.axis_index("y")) * C + core
    tiles_dev = rows_dev // TILE
    spread = tok_dev // TILE
    total_tiles = tiles_dev * groups
    capacity = max(2, (tiles_dev + groups - 1) // groups)
    slot_rows = groups * capacity * TILE

    target = tile_pos // spread
    local_pos = tile_pos - group_index * spread
    tile_index = jnp.arange(total_tiles, dtype=jnp.int32)
    source = tile_index // tiles_dev
    earlier = (
        (source[:, None] == source[None, :])
        & (target[:, None] == target[None, :])
        & (tile_index[:, None] < tile_index[None, :])
    )
    standing = jnp.sum(earlier.astype(jnp.int32), axis=0)

    def slots_of(names, rows, slot):
        row = jnp.arange(rows, dtype=jnp.int32)
        chosen = names[:, None] == (row // TILE)[None, :]
        found = slot[:, None] * TILE + (row % TILE)[None, :] + 1
        return jnp.sum(jnp.where(chosen, found, 0), axis=0) - 1

    doc_slot = slots_of(local_pos, tok_dev, source * capacity + standing)
    image_slot = slots_of(
        tile_index - group_index * tiles_dev, rows_dev, target * capacity + standing
    )
    receiver = match_table(doc_slot, slot_rows).astype(bf16)
    sender = match_table(image_slot, slot_rows).astype(bf16)

    def gathered(table, rows):
        return jnp.dot(table, rows, preferred_element_type=f32).astype(bf16)

    def scattered(table, rows):
        return lax.dot_general(table, rows, (((0,), (0,)), ((), ())), preferred_element_type=f32)

    def exchange(rows):
        split = rows.reshape(groups, capacity * TILE, local_cols)
        return swap_all(split, "grp").reshape(slot_rows, local_cols)

    fetch_out = gathered(receiver, d_normed)
    fetch_in = exchange(fetch_out)

    pair_weight = swap_pair(proj_weight)

    activated = gelu(hidden.astype(f32)).astype(bf16)
    image_rows = jnp.dot(activated, proj_weight, preferred_element_type=f32) + proj_bias
    image_rows = image_rows.astype(bf16)
    pair_rows = swap_pair(image_rows)

    late_sender, pair_rows = lax.optimization_barrier((sender, pair_rows))
    image_cot = scattered(late_sender, fetch_in).astype(bf16)
    image_grad = image_cot.astype(f32) * norm_gain
    pair_grad = swap_pair(image_grad)

    gain_row = norm_gain.reshape(1, local_cols)
    sums = row_sums(
        image_rows, pair_rows, image_grad, pair_grad, text_embed, d_normed, gain_row
    )
    sums = swap_all(sums, ("x", "y"))

    even, odd = here ^ 1, 3 - here
    shape = (X, Y, C, local_cols, local_cols)
    picks = (3 - even, even, odd ^ 1, odd, odd, here, even, here)
    image_normed, sent_a, sent_b, kept_a, kept_b = product(
        proj_weight.reshape(shape),
        pair_weight.reshape(shape),
        sums,
        (image_rows, pair_rows),
        (image_grad, pair_grad),
        gain_row,
        picks,
        core,
        model_width,
    )
    got_a = swap_even(sent_a)
    got_b = swap_odd(sent_b)

    def both(kept, got, index):
        return kept[index].astype(f32) + got[index].astype(f32)

    last_a = swap_odd(both(kept_a, got_a, 0).astype(bf16))
    last_b = swap_even(both(kept_b, got_b, 0).astype(bf16))
    over_x = combined(kept_a, got_a, last_a, kept_b, got_b, last_b)
    over_y = swap_all(over_x, "y")
    d_act = jnp.sum(over_y.astype(f32), axis=0).T
    own_hidden = lax.dynamic_slice_in_dim(hidden, lane_index * local_cols, local_cols, 1)
    d_hidden = (d_act * gelu_slope(own_hidden.astype(f32))).astype(bf16)

    outgoing = gathered(sender, image_normed)
    incoming = exchange(outgoing)
    placed = scattered(receiver, incoming).astype(bf16)

    text_sums = jnp.sum(sums[:, 2:], axis=0)
    text_sums = text_sums + swap_pair(text_sums)
    text_sq, text_cr = text_sums.reshape(2, tok_dev)
    inverse = lax.rsqrt(text_sq / model_width + epsilon)[:, None]
    cross_mean = (text_cr / model_width)[:, None]
    is_image = (doc_slot >= 0)[:, None]
    text_wide = text_embed.astype(f32)
    text_grad = d_normed.astype(f32) * norm_gain
    text_normed = (text_wide * inverse * norm_gain).astype(bf16)
    normed = jnp.where(is_image, placed, text_normed)
    d_text = inverse * (text_grad - text_wide * inverse * inverse * cross_mean)
    d_text = jnp.where(is_image, 0.0, d_text).astype(bf16)
    return (normed, d_text, d_hidden)


def solution(mesh):
    groups = mesh.shape["grp"]
    fine = Mesh(mesh.devices.reshape(groups, X, Y, C), ("grp", "x", "y", "core"))
    tp = ("x", "y", "core")
    in_specs = (
        P("grp", None),
        P(None, tp),
        P(tp),
        P(),
        P("grp", tp),
        P(tp),
        P("grp", tp),
    )
    out_specs = (P("grp", tp), P("grp", tp), P("grp", tp))

    return jax.shard_map(on_device, mesh=fine, in_specs=in_specs, out_specs=out_specs, check_vma=False)
```

time: 223 us -> 119 us (0.53)
  the two profiles are of different devices: /device:TPU:64 before, /device:TPU:16 now
where the time goes in v1:
time: 119 us; the launch traced here: 118 us
  starting transfers between devices  55.2 us (46%)
  waiting for transfers between devices  36.4 us (31%)
  Pallas kernels  10.4 us (9%)
  matrix products  9.13 us (8%)
  other arithmetic  4.09 us (3%)
  local copies, waits for them, and re-layouts  1.89 us (2%)
    all_to_all x4, starting transfers between devices, swap_all(): return lax.all_to_all(value, axis, split_axis=0, concat_axis=0, tiled=True)  37.1 us
    all_to_all x4, waiting for transfers between devices, swap_all(): return lax.all_to_all(value, axis, split_axis=0, concat_axis=0, tiled=True)  25.1 us
    pallas_call x1, Pallas kernels, product(): pl.pallas_call(kernel, grid_spec=pltpu.PrefetchScalarGridSpec(num_scalar_...  8.29 us
    ppermute x2, waiting for transfers between devices, swap_odd(): return lax.ppermute(value, 'x', [(i, 3 - i) for i in range(X)])  8.24 us
    ppermute x4, starting transfers between devices, swap_pair(): return lax.ppermute(value, 'core', [(0, 1), (1, 0)])  7.89 us
    ppermute x2, starting transfers between devices, swap_odd(): return lax.ppermute(value, 'x', [(i, 3 - i) for i in range(X)])  6.38 us
    dot_general x1, matrix products, on_device(): jnp.dot(activated, proj_weight, preferred_element_type=f32) + proj_bias  4.62 us
    ppermute x2, starting transfers between devices, swap_even(): return lax.ppermute(value, 'x', [(i, i ^ 1) for i in range(X)])  3.88 us
  transfers between devices with their start and end apart: 12, of which 9 were waited for; matrix products, arithmetic and copies ran while one was open for 12% of the time, Pallas kernels for 2%

profile of v1, /device:TPU:16, one launch (start us, length us, event | category | flops | bytes accessed | tf_op | source)
XLA Modules:
  0.0 118.0 jit_solution(6173872063202649289)
XLA Ops:
  0.6 1.9 %collective-permute-start = (bf16[8192,256]{1,0:T(8,128)(2,1)}, bf16[8192,256]{1,0:T(8,128)(2,1)}, u32[]{:S(2)}, u32[]{:S(2)}) collective-permute-start(bf16[8192,256]{1,0:T(8,128)(2,1)} %param.8), channel_id=1, source_target_pairs={{0,1},{1,0},{2,3},{3,2},{4,5},{5,4},{6,7},{7,6},{8,9},{9,8},{10,11... | collective-permute-start | bytes 12582920 | tf_op jit(solution)/shard_map/ppermute | solution.py:170
  2.6 0.7 add_select_fusion
  3.7 0.7 broadcast_subtract_fusion
  4.8 2.0 %fusion.9 = bf16[384,256]{1,0:T(8,128)(2,1)} fusion(bf16[768,256]{1,0:T(8,128)(2,1)} %d_r.1, s32[768]{0:T(1024)S(1)} %broadcast_add_fusion), kind=kOutput, calls=%fused_computation.15 | convolution fusion | flops 151388160 | bytes 592896 | tf_op jit(solution)/shard_map/dot_general | solution.py:225
  6.8 16.4 %all-to-all-start = ((bf16[24,16,256]{2,1,0:T(8,128)(2,1)}), bf16[24,16,256]{2,1,0:T(8,128)(2,1)S(1)}, u32[]{:S(2)}, u32[]{:S(2)}) async-start(bf16[24,16,256]{2,1,0:T(8,128)(2,1)} %bitcast.8), calls=%async_computation | async-start | bytes 393216 | tf_op jit(solution)/shard_map/all_to_all | solution.py:182
  23.3 4.6 %fusion.13.image_r.own_r = bf16[256,256]{1,0:T(8,128)(2,1)S(1)} fusion(bf16[8192,256]{1,0:T(8,128)(2,1)} %param.8, bf16[256,8192]{1,0:T(8,128)(2,1)} %param.7, f32[256]{0:T(256)} %param.9), kind=kOutput, calls=%fused_computation.18 | convolution fusion | flops 1086455808 | bytes 8520704 | tf_op jit(solution)/shard_map/dot_general | solution.py:240
  27.9 2.1 %collective-permute-start.1 = (bf16[256,256]{1,0:T(8,128)(2,1)S(1)}, bf16[256,256]{1,0:T(8,128)(2,1)S(1)}, u32[]{:S(2)}, u32[]{:S(2)}) collective-permute-start(bf16[256,256]{1,0:T(8,128)(2,1)S(1)} %fusion.13.image_r.own_r), channel_id=1, source_target_pairs={{0,1},{1,0},{2,3},{3,2},{4,5},{5,4},{6,7},{7,6},{8,9},{9,8},{10,11... | collective-permute-start | bytes 393224 | tf_op jit(solution)/shard_map/ppermute | solution.py:170
  30.4 0.7 collective-permute-done.1.pair_r
  31.1 6.9 %all-to-all-done = bf16[24,16,256]{2,1,0:T(8,128)(2,1)S(1)} async-done(((bf16[24,16,256]{2,1,0:T(8,128)(2,1)}), bf16[24,16,256]{2,1,0:T(8,128)(2,1)S(1)}, u32[]{:S(2)}, u32[]{:S(2)}) %all-to-all-start) | async-done | bytes 196640 | tf_op jit(solution)/shard_map/all_to_all | solution.py:182
  38.3 1.9 %collective-permute-start.2 = (f32[256,256]{1,0:T(8,128)S(1)}, f32[256,256]{1,0:T(8,128)S(1)}, u32[]{:S(2)}, u32[]{:S(2)}) collective-permute-start(f32[256,256]{1,0:T(8,128)S(1)} %fusion.17.image_g.own_g), channel_id=1, source_target_pairs={{0,1},{1,0},{2,3},{3,2},{4,5},{5,4},{6,7},{7,6},{8,9},{9,8},{10,11... | collective-permute-start | bytes 786440 | tf_op jit(solution)/shard_map/ppermute | solution.py:170
  40.3 1.5 %collective-permute-done.2.pair_g = f32[256,256]{1,0:T(8,128)S(1)} collective-permute-done((f32[256,256]{1,0:T(8,128)S(1)}, f32[256,256]{1,0:T(8,128)S(1)}, u32[]{:S(2)}, u32[]{:S(2)}) %collective-permute-start.2) | collective-permute-done | bytes 262176 | tf_op jit(solution)/shard_map/ppermute | solution.py:170
  41.8 1.1 shard_map.94
  42.9 9.0 %all-to-all-start.1 = ((f32[16,8,256]{2,1,0:T(8,128)}), f32[16,8,256]{2,1,0:T(8,128)S(1)}, u32[]{:S(2)}, u32[]{:S(2)}) async-start(f32[16,8,256]{2,1,0:T(8,128)} %shard_map.94), calls=%async_computation.1 | async-start | bytes 262144 | tf_op jit(solution)/shard_map/all_to_all | solution.py:182
  52.0 8.6 %all-to-all-done.1.sums_r = f32[16,8,256]{2,1,0:T(8,128)S(1)} async-done(((f32[16,8,256]{2,1,0:T(8,128)}), f32[16,8,256]{2,1,0:T(8,128)S(1)}, u32[]{:S(2)}, u32[]{:S(2)}) %all-to-all-start.1) | async-done | bytes 131104 | tf_op jit(solution)/shard_map/all_to_all | solution.py:182
  60.6 8.3 %shard_map.95 = (bf16[256,256]{1,0:T(8,128)(2,1)S(1)}, bf16[2,2,256,256]{3,2,1,0:T(8,128)(2,1)}, bf16[2,2,256,256]{3,2,1,0:T(8,128)(2,1)}, bf16[2,2,256,256]{3,2...) custom-call(s32[9]{0:T(128)S(1)} %stack.30.pick, bf16[4,4,2,256,256]{4,3,2,1,0:T(8,128)(2,1)} %bitcast.29, ...), custom_call_target="tpu_custom_call" | custom-call | flops 1073741824 | bytes 6291456 | tf_op jit(solution)/shard_map/pallas_call | solution.py:122
  68.8 3.0 %collective-permute-start.6 = (bf16[2,2,256,256]{3,2,1,0:T(8,128)(2,1)}, bf16[2,2,256,256]{3,2,1,0:T(8,128)(2,1)S(1)}, u32[]{:S(2)}, u32[]{:S(2)}) collective-permute-start(bf16[2,2,256,256]{3,2,1,0:T(8,128)(2,1)} %get-tuple-element.16), channel_id=1, source_target_pairs={{0,24},{8,16},{16,8},{24,0},{1,25},{9,17},{17,9},{25,1},{2,26},{10... | collective-permute-start | bytes 1572872 | tf_op jit(solution)/shard_map/ppermute | solution.py:178
  71.8 2.0 %collective-permute-start.4 = (bf16[2,2,256,256]{3,2,1,0:T(8,128)(2,1)}, bf16[2,2,256,256]{3,2,1,0:T(8,128)(2,1)S(1)}, u32[]{:S(2)}, u32[]{:S(2)}) collective-permute-start(bf16[2,2,256,256]{3,2,1,0:T(8,128)(2,1)} %get-tuple-element.14), channel_id=1, source_target_pairs={{0,8},{8,0},{16,24},{24,16},{1,9},{9,1},{17,25},{25,17},{2,10},{10... | collective-permute-start | bytes 1572872 | tf_op jit(solution)/shard_map/ppermute | solution.py:174
  73.8 0.9 convolution_convert_fusion.1
  74.7 4.6 %all-to-all-start.2 = ((bf16[24,16,256]{2,1,0:T(8,128)(2,1)}), bf16[24,16,256]{2,1,0:T(8,128)(2,1)S(1)}, u32[]{:S(2)}, u32[]{:S(2)}) async-start(bf16[24,16,256]{2,1,0:T(8,128)(2,1)} %bitcast.11), calls=%async_computation.2 | async-start | bytes 393216 | tf_op jit(solution)/shard_map/all_to_all | solution.py:182
  79.3 4.9 %collective-permute-done.6.got_b = bf16[2,2,256,256]{3,2,1,0:T(8,128)(2,1)S(1)} collective-permute-done((bf16[2,2,256,256]{3,2,1,0:T(8,128)(2,1)}, bf16[2,2,256,256]{3,2,1,0:T(8,128)(2,1)S(1)}, u32[]{:S(2)}, u32[]{:S(2)}) %collective-permute-start.6) | collective-permute-done | bytes 524320 | tf_op jit(solution)/shard_map/ppermute | solution.py:178
  84.3 1.9 %collective-permute-start.7 = (bf16[2,256,256]{2,1,0:T(8,128)(2,1)S(1)}, bf16[2,256,256]{2,1,0:T(8,128)(2,1)S(1)}, u32[]{:S(2)}, u32[]{:S(2)}) collective-permute-start(bf16[2,256,256]{2,1,0:T(8,128)(2,1)S(1)} %fusion.29), channel_id=1, source_target_pairs={{0,8},{8,0},{16,24},{24,16},{1,9},{9,1},{17,25},{25,17},{2,10},{10... | collective-permute-start | bytes 786440 | tf_op jit(solution)/shard_map/ppermute | solution.py:174
  86.4 3.4 %collective-permute-start.5 = (bf16[2,256,256]{2,1,0:T(8,128)(2,1)S(1)}, bf16[2,256,256]{2,1,0:T(8,128)(2,1)S(1)}, u32[]{:S(2)}, u32[]{:S(2)}) collective-permute-start(bf16[2,256,256]{2,1,0:T(8,128)(2,1)S(1)} %fusion.28), channel_id=1, source_target_pairs={{0,24},{8,16},{16,8},{24,0},{1,25},{9,17},{17,9},{25,1},{2,26},{10... | collective-permute-start | bytes 786440 | tf_op jit(solution)/shard_map/ppermute | solution.py:178
  89.9 1.9 %collective-permute-start.3 = (f32[6,256]{1,0:T(8,128)S(1)}, f32[6,256]{1,0:T(8,128)S(1)}, u32[]{:S(2)}, u32[]{:S(2)}) collective-permute-start(f32[6,256]{1,0:T(8,128)S(1)} %slice_reduce_fusion), channel_id=1, source_target_pairs={{0,1},{1,0},{2,3},{3,2},{4,5},{5,4},{6,7},{7,6},{8,9},{9,8},{10,11... | collective-permute-start | bytes 18440 | tf_op jit(solution)/shard_map/ppermute | solution.py:170
  91.8 0.7 collective-permute-done.7.last_b
  92.5 3.4 %collective-permute-done.5.last_a = bf16[2,256,256]{2,1,0:T(8,128)(2,1)S(1)} collective-permute-done((bf16[2,256,256]{2,1,0:T(8,128)(2,1)S(1)}, bf16[2,256,256]{2,1,0:T(8,128)(2,1)S(1)}, u32[]{:S(2)}, u32[]{:S(2)}) %collective-permute-start.5) | collective-permute-done | bytes 262176 | tf_op jit(solution)/shard_map/ppermute | solution.py:178
  95.9 1.0 shard_map.96
  96.9 7.1 %all-to-all-start.3 = ((bf16[4,256,256]{2,1,0:T(8,128)(2,1)}), bf16[4,256,256]{2,1,0:T(8,128)(2,1)S(1)}, u32[]{:S(2)}, u32[]{:S(2)}) async-start(bf16[4,256,256]{2,1,0:T(8,128)(2,1)} %shard_map.96), calls=%async_computation.3 | async-start | bytes 1048576 | tf_op jit(solution)/shard_map/all_to_all | solution.py:182
  104.0 0.9 constant_dynamic-slice_fusion
  105.0 1.1 select_convert_fusion
  106.2 1.3 %fusion.7 = bf16[768,256]{1,0:T(8,128)(2,1)} fusion(bf16[384,256]{1,0:T(8,128)(2,1)S(1)} %bitcast.31, s32[768]{0:T(1024)S(1)} %broadcast_add_fusion, bf16[768,256]{1,0:T(8,128)(2,1)S(1)} %copy-done.1, f32[256]{0:T(256)S(1)} %copy-done.2, f32[768]{0:T(1024)S(1)} %rsqrt.11, pred[768]{0:T(1024)(128)(4,1)S(1)} %broadcast_compare_fusion), kind=kOutput, calls=%fused_computation.12 | convolution fusion | flops 152469504 | bytes 990976 | tf_op jit(solution)/shard_map/dot_general | solution.py:228
  107.5 9.6 %all-to-all-done.3 = bf16[4,256,256]{2,1,0:T(8,128)(2,1)S(1)} async-done(((bf16[4,256,256]{2,1,0:T(8,128)(2,1)}), bf16[4,256,256]{2,1,0:T(8,128)(2,1)S(1)}, u32[]{:S(2)}, u32[]{:S(2)}) %all-to-all-start.3) | async-done | bytes 524320 | tf_op jit(solution)/shard_map/all_to_all | solution.py:182
  117.3 0.8 copy.13
  (32 shorter events, 2.2 us)
Async XLA Ops:
  0.6 59.9 %collective-permute-start = (bf16[8192,256]{1,0:T(8,128)(2,1)}, bf16[8192,256]{1,0:T(8,128)(2,1)}, u32[]{:S(2)}, u32[]{:S(2)}) collective-permute-start(bf16[8192,256]{1,0:T(8,128)(2,1)} %param.8), channel_id=1, source_target_pairs={{0,1},{1,0},{2,3},{3,2},{4,5},{5,4},{6,7},{7,6},{8,9},{9,8},{10,11... | collective-permute-start | bytes 12582920 | tf_op jit(solution)/shard_map/ppermute | solution.py:170
  6.8 31.2 %all-to-all-start = ((bf16[24,16,256]{2,1,0:T(8,128)(2,1)}), bf16[24,16,256]{2,1,0:T(8,128)(2,1)S(1)}, u32[]{:S(2)}, u32[]{:S(2)}) async-start(bf16[24,16,256]{2,1,0:T(8,128)(2,1)} %bitcast.8), calls=%async_computation | async-start | bytes 393216 | tf_op jit(solution)/shard_map/all_to_all | solution.py:182
  23.2 14.8 %copy-start.2 = (f32[256]{0:T(256)S(1)}, f32[256]{0:T(256)}, u32[]{:S(2)}) copy-start(f32[256]{0:T(256)} %param.12) | copy-start | bytes 3076
  23.2 18.5 %copy-start = (bf16[768,256]{1,0:T(8,128)(2,1)S(1)}, bf16[768,256]{1,0:T(8,128)(2,1)}, u32[]{:S(2)}) copy-start(bf16[768,256]{1,0:T(8,128)(2,1)} %d_r.1) | copy-start | bytes 1179652
  23.3 18.5 %copy-start.1 = (bf16[768,256]{1,0:T(8,128)(2,1)S(1)}, bf16[768,256]{1,0:T(8,128)(2,1)}, u32[]{:S(2)}) copy-start(bf16[768,256]{1,0:T(8,128)(2,1)} %text_r.1) | copy-start | bytes 1179652
  27.9 3.2 %collective-permute-start.1 = (bf16[256,256]{1,0:T(8,128)(2,1)S(1)}, bf16[256,256]{1,0:T(8,128)(2,1)S(1)}, u32[]{:S(2)}, u32[]{:S(2)}) collective-permute-start(bf16[256,256]{1,0:T(8,128)(2,1)S(1)} %fusion.13.image_r.own_r), channel_id=1, source_target_pairs={{0,1},{1,0},{2,3},{3,2},{4,5},{5,4},{6,7},{7,6},{8,9},{9,8},{10,11... | collective-permute-start | bytes 393224 | tf_op jit(solution)/shard_map/ppermute | solution.py:170
  38.3 3.4 %collective-permute-start.2 = (f32[256,256]{1,0:T(8,128)S(1)}, f32[256,256]{1,0:T(8,128)S(1)}, u32[]{:S(2)}, u32[]{:S(2)}) collective-permute-start(f32[256,256]{1,0:T(8,128)S(1)} %fusion.17.image_g.own_g), channel_id=1, source_target_pairs={{0,1},{1,0},{2,3},{3,2},{4,5},{5,4},{6,7},{7,6},{8,9},{9,8},{10,11... | collective-permute-start | bytes 786440 | tf_op jit(solution)/shard_map/ppermute | solution.py:170
  42.9 17.7 %all-to-all-start.1 = ((f32[16,8,256]{2,1,0:T(8,128)}), f32[16,8,256]{2,1,0:T(8,128)S(1)}, u32[]{:S(2)}, u32[]{:S(2)}) async-start(f32[16,8,256]{2,1,0:T(8,128)} %shard_map.94), calls=%async_computation.1 | async-start | bytes 262144 | tf_op jit(solution)/shard_map/all_to_all | solution.py:182
  68.8 15.3 %collective-permute-start.6 = (bf16[2,2,256,256]{3,2,1,0:T(8,128)(2,1)}, bf16[2,2,256,256]{3,2,1,0:T(8,128)(2,1)S(1)}, u32[]{:S(2)}, u32[]{:S(2)}) collective-permute-start(bf16[2,2,256,256]{3,2,1,0:T(8,128)(2,1)} %get-tuple-element.16), channel_id=1, source_target_pairs={{0,24},{8,16},{16,8},{24,0},{1,25},{9,17},{17,9},{25,1},{2,26},{10... | collective-permute-start | bytes 1572872 | tf_op jit(solution)/shard_map/ppermute | solution.py:178
  71.8 14.5 %collective-permute-start.4 = (bf16[2,2,256,256]{3,2,1,0:T(8,128)(2,1)}, bf16[2,2,256,256]{3,2,1,0:T(8,128)(2,1)S(1)}, u32[]{:S(2)}, u32[]{:S(2)}) collective-permute-start(bf16[2,2,256,256]{3,2,1,0:T(8,128)(2,1)} %get-tuple-element.14), channel_id=1, source_target_pairs={{0,8},{8,0},{16,24},{24,16},{1,9},{9,1},{17,25},{25,17},{2,10},{10... | collective-permute-start | bytes 1572872 | tf_op jit(solution)/shard_map/ppermute | solution.py:174
  74.7 22.2 %all-to-all-start.2 = ((bf16[24,16,256]{2,1,0:T(8,128)(2,1)}), bf16[24,16,256]{2,1,0:T(8,128)(2,1)S(1)}, u32[]{:S(2)}, u32[]{:S(2)}) async-start(bf16[24,16,256]{2,1,0:T(8,128)(2,1)} %bitcast.11), calls=%async_computation.2 | async-start | bytes 393216 | tf_op jit(solution)/shard_map/all_to_all | solution.py:182
  84.3 8.3 %collective-permute-start.7 = (bf16[2,256,256]{2,1,0:T(8,128)(2,1)S(1)}, bf16[2,256,256]{2,1,0:T(8,128)(2,1)S(1)}, u32[]{:S(2)}, u32[]{:S(2)}) collective-permute-start(bf16[2,256,256]{2,1,0:T(8,128)(2,1)S(1)} %fusion.29), channel_id=1, source_target_pairs={{0,8},{8,0},{16,24},{24,16},{1,9},{9,1},{17,25},{25,17},{2,10},{10... | collective-permute-start | bytes 786440 | tf_op jit(solution)/shard_map/ppermute | solution.py:174
  86.4 9.5 %collective-permute-start.5 = (bf16[2,256,256]{2,1,0:T(8,128)(2,1)S(1)}, bf16[2,256,256]{2,1,0:T(8,128)(2,1)S(1)}, u32[]{:S(2)}, u32[]{:S(2)}) collective-permute-start(bf16[2,256,256]{2,1,0:T(8,128)(2,1)S(1)} %fusion.28), channel_id=1, source_target_pairs={{0,24},{8,16},{16,8},{24,0},{1,25},{9,17},{17,9},{25,1},{2,26},{10... | collective-permute-start | bytes 786440 | tf_op jit(solution)/shard_map/ppermute | solution.py:178
  89.9 15.1 %collective-permute-start.3 = (f32[6,256]{1,0:T(8,128)S(1)}, f32[6,256]{1,0:T(8,128)S(1)}, u32[]{:S(2)}, u32[]{:S(2)}) collective-permute-start(f32[6,256]{1,0:T(8,128)S(1)} %slice_reduce_fusion), channel_id=1, source_target_pairs={{0,1},{1,0},{2,3},{3,2},{4,5},{5,4},{6,7},{7,6},{8,9},{9,8},{10,11... | collective-permute-start | bytes 18440 | tf_op jit(solution)/shard_map/ppermute | solution.py:170
  96.9 20.2 %all-to-all-start.3 = ((bf16[4,256,256]{2,1,0:T(8,128)(2,1)}), bf16[4,256,256]{2,1,0:T(8,128)(2,1)S(1)}, u32[]{:S(2)}, u32[]{:S(2)}) async-start(bf16[4,256,256]{2,1,0:T(8,128)(2,1)} %shard_map.96), calls=%async_computation.3 | async-start | bytes 1048576 | tf_op jit(solution)/shard_map/all_to_all | solution.py:182

commit v2 on v1

--- a/solution.py
+++ b/solution.py
@@ -30,21 +30,21 @@
     return wanted[None, :] == jnp.arange(choices_count, dtype=jnp.int32)[:, None]
 
 
-def row_sums(image_rows, pair_rows, image_grad, pair_grad, text_embed, d_normed, norm_gain):
+def row_sums(image_rows, image_grad, text_embed, d_normed, norm_gain):
     rows, cols = image_rows.shape
     texts = text_embed.shape[0] // rows
     count = 2 + 2 * texts
 
-    def kernel(image_r, pair_r, image_g, pair_g, text_r, d_r, gain_r, o_ref):
+    def kernel(image_r, image_g, text_r, d_r, gain_r, o_ref):
         lane = lax.broadcasted_iota(jnp.int32, (rows, LANES), 1)
         table = jnp.zeros((rows, LANES), f32)
 
         def put(table, index, values):
             return jnp.where(lane == index, jnp.sum(values, axis=1, keepdims=True), table)
 
-        wide, pair = image_r[...].astype(f32), pair_r[...].astype(f32)
-        table = put(table, 0, wide * wide + pair * pair)
-        table = put(table, 1, image_g[...] * wide + pair_g[...] * pair)
+        wide = image_r[...].astype(f32)
+        table = put(table, 0, wide * wide)
+        table = put(table, 1, image_g[...] * wide)
         for i in range(texts):
             text = text_r[pl.ds(i * rows, rows), :].astype(f32)
             grad = d_r[pl.ds(i * rows, rows), :].astype(f32) * gain_r[...]
@@ -58,25 +58,26 @@
         out_shape=jax.ShapeDtypeStruct((X * Y, count, rows), f32),
         compiler_params=pltpu.CompilerParams(vmem_limit_bytes=GRANT),
         cost_estimate=pl.CostEstimate(
-            flops=8 * rows * cols * (texts + 2), bytes_accessed=4 * rows * cols * (texts + 3), transcendentals=0
-        ),
-    )(image_rows, pair_rows, image_grad, pair_grad, text_embed, d_normed, norm_gain)
-
-
-def product(own_weight, pair_weight, sums, rows_pair, grads_pair, norm_gain, picks, core, width):
+            flops=8 * rows * cols * (texts + 2),
+            bytes_accessed=4 * rows * cols * (texts + 2),
+            transcendentals=0,
+        ),
+    )(image_rows, image_grad, text_embed, d_normed, norm_gain)
+
+
+def product(own_weight, pair_weight, sums_pair, rows_pair, grads_pair, norm_gain, picks, core, width):
     features, cols = own_weight.shape[-2:]
     rows = rows_pair[0].shape[0]
     half = Y // 2
     groups, each = 4, 2
-    steps = groups * each
-
-    def kernel(pick, own_w, pair_w, sums_r, own_r, pair_r, own_g, pair_g, gain, *rest):
+
+    def kernel(pick, own_0, own_1, pair_0, pair_1, own_s, pair_s, own_r, pair_r, own_g, pair_g, gain, *rest):
         normed, outs, own_d, pair_d = rest[0], rest[1:5], rest[5], rest[6]
         step = pl.program_id(0)
 
         @pl.when(step == 0)
         def _():
-            total = jnp.sum(sums_r[...], axis=0)
+            total = own_s[...] + pair_s[...]
             full = jnp.concatenate([total, jnp.zeros((LANES - total.shape[0], rows), f32)], axis=0)
             columns = full.T
             inverse = lax.rsqrt(columns[:, 0:1] / width + epsilon)
@@ -84,61 +85,81 @@
 
             def gradient(wide, grad):
                 d_rows = inverse * (grad - wide * inverse * inverse * cross_mean)
-                return d_rows.astype(bf16)
+                return d_rows.T.astype(bf16)
 
             wide = own_r[...].astype(f32)
             own_d[...] = gradient(wide, own_g[...])
             pair_d[...] = gradient(pair_r[...].astype(f32), pair_g[...])
             normed[...] = (wide * inverse * gain[...]).astype(bf16)
 
-        def part(w, g):
-            return lax.dot_general(
-                w[...].reshape(half * features, cols),
-                g[...],
-                (((1,), (1,)), ((), ())),
-                preferred_element_type=f32,
-            )
-
-        total = part(own_w, own_d) + part(pair_w, pair_d)
-        total = total.astype(bf16).reshape(1, half, features, rows)
+        def part(w, d):
+            return jnp.dot(w[...].reshape(half * features, cols), d[...], preferred_element_type=f32)
+
+        totals = [
+            (part(own, own_d) + part(pair, pair_d)).astype(bf16).reshape(half, features, rows)
+            for own, pair in ((own_0, pair_0), (own_1, pair_1))
+        ]
         for k, out in enumerate(outs):
 
-            @pl.when(step // each == k)
+            @pl.when(step == k)
             def _(out=out):
-                out[...] = total
+                for j, total in enumerate(totals):
+                    out[j] = total
 
     def whole(*shape):
         return pl.BlockSpec(shape, lambda i, s: (0,) * len(shape))
 
-    weight_spec = pl.BlockSpec(
-        (None, half, None, features, cols), lambda i, s: (s[i], (i // each) % 2, s[steps], 0, 0)
-    )
-
-    def out_spec(k):
+    def weight_spec(j):
         return pl.BlockSpec(
-            (1, half, features, rows), lambda i, s: (jnp.clip(i - each * k, 0, each - 1), 0, 0, 0)
+            (None, half, None, features, cols),
+            lambda i, s: (s[each * i + j], i % 2, s[groups * each], 0, 0),
         )
 
     return pl.pallas_call(
         kernel,
         grid_spec=pltpu.PrefetchScalarGridSpec(
             num_scalar_prefetch=1,
-            grid=(steps,),
-            in_specs=[weight_spec, weight_spec, whole(*sums.shape)]
+            grid=(groups,),
+            in_specs=[weight_spec(0), weight_spec(1)] * 2
+            + [whole(*sums_pair[0].shape)] * 2
             + [whole(rows, cols)] * 4
             + [whole(1, cols)],
-            out_specs=[whole(rows, cols)] + [out_spec(k) for k in range(groups)],
-            scratch_shapes=[pltpu.VMEM((rows, cols), bf16)] * 2,
+            out_specs=[whole(rows, cols)] + [whole(each, half, features, rows)] * groups,
+            scratch_shapes=[pltpu.VMEM((cols, rows), bf16)] * 2,
         ),
         out_shape=[jax.ShapeDtypeStruct((rows, cols), bf16)]
         + [jax.ShapeDtypeStruct((each, half, features, rows), bf16)] * groups,
         compiler_params=pltpu.CompilerParams(vmem_limit_bytes=LARGE_GRANT),
         cost_estimate=pl.CostEstimate(
-            flops=4 * steps * half * features * cols * rows,
-            bytes_accessed=2 * steps * half * features * (2 * cols + rows),
+            flops=4 * groups * each * half * features * cols * rows,
+            bytes_accessed=2 * groups * each * half * features * (2 * cols + rows),
             transcendentals=rows,
         ),
-    )(jnp.stack([*picks, core]), own_weight, pair_weight, sums, *rows_pair, *grads_pair, norm_gain)
+    )(
+        jnp.stack([*picks, core]),
+        *(own_weight, own_weight, pair_weight, pair_weight),
+        *sums_pair,
+        *rows_pair,
+        *grads_pair,
+        norm_gain,
+    )
+
+
+def finished(over_y, slope):
+    rows, cols = slope.shape
+
+    def kernel(parts, slope_r, o_ref):
+        total = jnp.sum(parts[...].astype(f32), axis=0)
+        o_ref[...] = (total.T * slope_r[...]).astype(bf16)
+
+    return pl.pallas_call(
+        kernel,
+        out_shape=jax.ShapeDtypeStruct((rows, cols), bf16),
+        compiler_params=pltpu.CompilerParams(vmem_limit_bytes=GRANT),
+        cost_estimate=pl.CostEstimate(
+            flops=6 * rows * cols, bytes_accessed=14 * rows * cols, transcendentals=0
+        ),
+    )(over_y, slope)
 
 
 def combined(kept_a, got_a, last_a, kept_b, got_b, last_b):
@@ -239,18 +260,16 @@
     activated = gelu(hidden.astype(f32)).astype(bf16)
     image_rows = jnp.dot(activated, proj_weight, preferred_element_type=f32) + proj_bias
     image_rows = image_rows.astype(bf16)
+
+    image_cot = scattered(sender, fetch_in).astype(bf16)
+    image_grad = image_cot.astype(f32) * norm_gain
+
+    gain_row = norm_gain.reshape(1, local_cols)
+    copies = row_sums(image_rows, image_grad, text_embed, d_normed, gain_row)
+    sums = jnp.sum(swap_all(copies, ("x", "y")), axis=0)
+    pair_sums = swap_pair(sums)
     pair_rows = swap_pair(image_rows)
-
-    late_sender, pair_rows = lax.optimization_barrier((sender, pair_rows))
-    image_cot = scattered(late_sender, fetch_in).astype(bf16)
-    image_grad = image_cot.astype(f32) * norm_gain
     pair_grad = swap_pair(image_grad)
-
-    gain_row = norm_gain.reshape(1, local_cols)
-    sums = row_sums(
-        image_rows, pair_rows, image_grad, pair_grad, text_embed, d_normed, gain_row
-    )
-    sums = swap_all(sums, ("x", "y"))
 
     even, odd = here ^ 1, 3 - here
     shape = (X, Y, C, local_cols, local_cols)
@@ -258,7 +277,7 @@
     image_normed, sent_a, sent_b, kept_a, kept_b = product(
         proj_weight.reshape(shape),
         pair_weight.reshape(shape),
-        sums,
+        (sums, pair_sums),
         (image_rows, pair_rows),
         (image_grad, pair_grad),
         gain_row,
@@ -276,16 +295,15 @@
     last_b = swap_even(both(kept_b, got_b, 0).astype(bf16))
     over_x = combined(kept_a, got_a, last_a, kept_b, got_b, last_b)
     over_y = swap_all(over_x, "y")
-    d_act = jnp.sum(over_y.astype(f32), axis=0).T
     own_hidden = lax.dynamic_slice_in_dim(hidden, lane_index * local_cols, local_cols, 1)
-    d_hidden = (d_act * gelu_slope(own_hidden.astype(f32))).astype(bf16)
+    slope = gelu_slope(own_hidden.astype(f32))
+    d_hidden = finished(over_y, slope)
 
     outgoing = gathered(sender, image_normed)
     incoming = exchange(outgoing)
     placed = scattered(receiver, incoming).astype(bf16)
 
-    text_sums = jnp.sum(sums[:, 2:], axis=0)
-    text_sums = text_sums + swap_pair(text_sums)
+    text_sums = (sums + pair_sums)[2:]
     text_sq, text_cr = text_sums.reshape(2, tok_dev)
     inverse = lax.rsqrt(text_sq / model_width + epsilon)[:, None]
     cross_mean = (text_cr / model_width)[:, None]

time: 119 us -> 129 us (1.084)
  the two profiles are of different devices: /device:TPU:16 before, /device:TPU:8 now
where the time goes in v2:
time: 129 us; the launch traced here: 128 us
  starting transfers between devices  52 us (40%)
  waiting for transfers between devices  49.1 us (38%)
  matrix products  10.7 us (8%)
  Pallas kernels  8.78 us (7%)
  other arithmetic  6.26 us (5%)
    all_to_all x4, starting transfers between devices, swap_all(): return lax.all_to_all(value, axis, split_axis=0, concat_axis=0, tiled=True)  34.3 us
    all_to_all x4, waiting for transfers between devices, swap_all(): return lax.all_to_all(value, axis, split_axis=0, concat_axis=0, tiled=True)  34.2 us
    ppermute x2, waiting for transfers between devices, swap_odd(): return lax.ppermute(value, 'x', [(i, 3 - i) for i in range(X)])  9.95 us
    ppermute x4, starting transfers between devices, swap_pair(): return lax.ppermute(value, 'core', [(0, 1), (1, 0)])  8.02 us
    pallas_call x1, Pallas kernels, product(): pl.pallas_call(kernel, grid_spec=pltpu.PrefetchScalarGridSpec(num_scalar_...  5.95 us
    ppermute x2, starting transfers between devices, swap_odd(): return lax.ppermute(value, 'x', [(i, 3 - i) for i in range(X)])  5.83 us
    dot_general x1, matrix products, on_device(): jnp.dot(activated, proj_weight, preferred_element_type=f32) + proj_bias  4.57 us
    ppermute x2, waiting for transfers between devices, swap_even(): return lax.ppermute(value, 'x', [(i, i ^ 1) for i in range(X)])  3.92 us
  transfers between devices with their start and end apart: 12, of which 7 were waited for; matrix products, arithmetic and copies ran while one was open for 13% of the time, Pallas kernels for 2%

profile of v2, /device:TPU:8, one launch (start us, length us, event | category | flops | bytes accessed | tf_op | source)
XLA Modules:
  0.0 127.9 jit_solution(4789060352501247085)
XLA Ops:
  0.6 1.9 %collective-permute-start = (bf16[8192,256]{1,0:T(8,128)(2,1)}, bf16[8192,256]{1,0:T(8,128)(2,1)}, u32[]{:S(2)}, u32[]{:S(2)}) collective-permute-start(bf16[8192,256]{1,0:T(8,128)(2,1)} %param.8), channel_id=1, source_target_pairs={{0,1},{1,0},{2,3},{3,2},{4,5},{5,4},{6,7},{7,6},{8,9},{9,8},{10,11... | collective-permute-start | bytes 12582920 | tf_op jit(solution)/shard_map/ppermute | solution.py:191
  4.8 2.0 %fusion.9 = bf16[384,256]{1,0:T(8,128)(2,1)} fusion(bf16[768,256]{1,0:T(8,128)(2,1)} %d_r.1, s32[768]{0:T(1024)S(1)} %broadcast_add_fusion), kind=kOutput, calls=%fused_computation.15 | convolution fusion | flops 151388160 | bytes 592896 | tf_op jit(solution)/shard_map/dot_general | solution.py:246
  6.8 16.7 %all-to-all-start = ((bf16[24,16,256]{2,1,0:T(8,128)(2,1)}), bf16[24,16,256]{2,1,0:T(8,128)(2,1)S(1)}, u32[]{:S(2)}, u32[]{:S(2)}) async-start(bf16[24,16,256]{2,1,0:T(8,128)(2,1)} %bitcast.8), calls=%async_computation | async-start | bytes 393216 | tf_op jit(solution)/shard_map/all_to_all | solution.py:203
  23.8 13.3 %all-to-all-done = bf16[24,16,256]{2,1,0:T(8,128)(2,1)S(1)} async-done(((bf16[24,16,256]{2,1,0:T(8,128)(2,1)}), bf16[24,16,256]{2,1,0:T(8,128)(2,1)S(1)}, u32[]{:S(2)}, u32[]{:S(2)}) %all-to-all-start) | async-done | bytes 196640 | tf_op jit(solution)/shard_map/all_to_all | solution.py:203
  37.2 1.0 fusion.17.image_g.own_g
  38.2 2.1 %collective-permute-start.3 = (f32[256,256]{1,0:T(8,128)S(1)}, f32[256,256]{1,0:T(8,128)S(1)}, u32[]{:S(2)}, u32[]{:S(2)}) collective-permute-start(f32[256,256]{1,0:T(8,128)S(1)} %fusion.17.image_g.own_g), channel_id=1, source_target_pairs={{0,1},{1,0},{2,3},{3,2},{4,5},{5,4},{6,7},{7,6},{8,9},{9,8},{10,11... | collective-permute-start | bytes 786440 | tf_op jit(solution)/shard_map/ppermute | solution.py:191
  40.2 4.6 %fusion.13.image_r.own_r = bf16[256,256]{1,0:T(8,128)(2,1)S(1)} fusion(bf16[8192,256]{1,0:T(8,128)(2,1)} %param.8, bf16[256,8192]{1,0:T(8,128)(2,1)} %param.7, f32[256]{0:T(256)} %param.9), kind=kOutput, calls=%fused_computation.18 | convolution fusion | flops 1086455808 | bytes 8520704 | tf_op jit(solution)/shard_map/dot_general | solution.py:261
  44.8 1.1 shard_map.94
  45.9 8.8 %all-to-all-start.1 = ((f32[16,8,256]{2,1,0:T(8,128)}), f32[16,8,256]{2,1,0:T(8,128)S(1)}, u32[]{:S(2)}, u32[]{:S(2)}) async-start(f32[16,8,256]{2,1,0:T(8,128)} %shard_map.94), calls=%async_computation.1 | async-start | bytes 262144 | tf_op jit(solution)/shard_map/all_to_all | solution.py:203
  54.7 2.1 %collective-permute-start.2 = (bf16[256,256]{1,0:T(8,128)(2,1)S(1)}, bf16[256,256]{1,0:T(8,128)(2,1)S(1)}, u32[]{:S(2)}, u32[]{:S(2)}) collective-permute-start(bf16[256,256]{1,0:T(8,128)(2,1)S(1)} %fusion.13.image_r.own_r), channel_id=1, source_target_pairs={{0,1},{1,0},{2,3},{3,2},{4,5},{5,4},{6,7},{7,6},{8,9},{9,8},{10,11... | collective-permute-start | bytes 393224 | tf_op jit(solution)/shard_map/ppermute | solution.py:191
  56.8 9.4 %all-to-all-done.1 = f32[16,8,256]{2,1,0:T(8,128)S(1)} async-done(((f32[16,8,256]{2,1,0:T(8,128)}), f32[16,8,256]{2,1,0:T(8,128)S(1)}, u32[]{:S(2)}, u32[]{:S(2)}) %all-to-all-start.1) | async-done | bytes 131104 | tf_op jit(solution)/shard_map/all_to_all | solution.py:203
  66.2 1.9 %collective-permute-start.1 = (f32[8,256]{1,0:T(8,128)S(1)}, f32[8,256]{1,0:T(8,128)S(1)}, u32[]{:S(2)}, u32[]{:S(2)}) collective-permute-start(f32[8,256]{1,0:T(8,128)S(1)} %reduce_sum.39.own_s), channel_id=1, source_target_pairs={{0,1},{1,0},{2,3},{3,2},{4,5},{5,4},{6,7},{7,6},{8,9},{9,8},{10,11... | collective-permute-start | bytes 24584 | tf_op jit(solution)/shard_map/ppermute | solution.py:191
  68.3 1.0 collective-permute-done.1.pair_s
  69.3 5.9 %shard_map.95 = (bf16[256,256]{1,0:T(8,128)(2,1)S(1)}, bf16[2,2,256,256]{3,2,1,0:T(8,128)(2,1)}, bf16[2,2,256,256]{3,2,1,0:T(8,128)(2,1)S(1)}, bf16[2,2,256,256]...) custom-call(s32[9]{0:T(128)S(1)} %stack.30.pick, bf16[4,4,2,256,256]{4,3,2,1,0:T(8,128)(2,1)} %bitcast.24, ...), custom_call_target="tpu_custom_call" | custom-call | flops 1073741824 | bytes 6291456 | tf_op jit(solution)/shard_map/pallas_call | solution.py:118
  75.3 2.8 %collective-permute-start.6 = (bf16[2,2,256,256]{3,2,1,0:T(8,128)(2,1)S(1)}, bf16[2,2,256,256]{3,2,1,0:T(8,128)(2,1)S(1)}, u32[]{:S(2)}, u32[]{:S(2)}) collective-permute-start(bf16[2,2,256,256]{3,2,1,0:T(8,128)(2,1)S(1)} %get-tuple-element.12), channel_id=1, source_target_pairs={{0,24},{8,16},{16,8},{24,0},{1,25},{9,17},{17,9},{25,1},{2,26},{10... | collective-permute-start | bytes 1572872 | tf_op jit(solution)/shard_map/ppermute | solution.py:199
  78.0 1.9 %collective-permute-start.4 = (bf16[2,2,256,256]{3,2,1,0:T(8,128)(2,1)}, bf16[2,2,256,256]{3,2,1,0:T(8,128)(2,1)S(1)}, u32[]{:S(2)}, u32[]{:S(2)}) collective-permute-start(bf16[2,2,256,256]{3,2,1,0:T(8,128)(2,1)} %get-tuple-element.10), channel_id=1, source_target_pairs={{0,8},{8,0},{16,24},{24,16},{1,9},{9,1},{17,25},{25,17},{2,10},{10... | collective-permute-start | bytes 1572872 | tf_op jit(solution)/shard_map/ppermute | solution.py:195
  80.0 0.9 convolution_convert_fusion.1
  80.9 5.4 %all-to-all-start.2 = ((bf16[24,16,256]{2,1,0:T(8,128)(2,1)}), bf16[24,16,256]{2,1,0:T(8,128)(2,1)}, u32[]{:S(2)}, u32[]{:S(2)}) async-start(bf16[24,16,256]{2,1,0:T(8,128)(2,1)} %bitcast.27), calls=%async_computation.2 | async-start | bytes 393216 | tf_op jit(solution)/shard_map/all_to_all | solution.py:203
  86.3 6.0 %collective-permute-done.6.got_b = bf16[2,2,256,256]{3,2,1,0:T(8,128)(2,1)S(1)} collective-permute-done((bf16[2,2,256,256]{3,2,1,0:T(8,128)(2,1)S(1)}, bf16[2,2,256,256]{3,2,1,0:T(8,128)(2,1)S(1)}, u32[]{:S(2)}, u32[]{:S(2)}) %collective-permute-start.6) | collective-permute-done | bytes 524320 | tf_op jit(solution)/shard_map/ppermute | solution.py:199
  92.4 0.8 fusion.27
  93.1 1.9 %collective-permute-start.7 = (bf16[2,256,256]{2,1,0:T(8,128)(2,1)}, bf16[2,256,256]{2,1,0:T(8,128)(2,1)S(1)}, u32[]{:S(2)}, u32[]{:S(2)}) collective-permute-start(bf16[2,256,256]{2,1,0:T(8,128)(2,1)} %fusion.27), channel_id=1, source_target_pairs={{0,8},{8,0},{16,24},{24,16},{1,9},{9,1},{17,25},{25,17},{2,10},{10... | collective-permute-start | bytes 786440 | tf_op jit(solution)/shard_map/ppermute | solution.py:195
  95.0 0.8 fusion.26
  95.8 3.1 %collective-permute-start.5 = (bf16[2,256,256]{2,1,0:T(8,128)(2,1)}, bf16[2,256,256]{2,1,0:T(8,128)(2,1)S(1)}, u32[]{:S(2)}, u32[]{:S(2)}) collective-permute-start(bf16[2,256,256]{2,1,0:T(8,128)(2,1)} %fusion.26), channel_id=1, source_target_pairs={{0,24},{8,16},{16,8},{24,0},{1,25},{9,17},{17,9},{25,1},{2,26},{10... | collective-permute-start | bytes 786440 | tf_op jit(solution)/shard_map/ppermute | solution.py:199
  98.9 3.9 %collective-permute-done.7.last_b = bf16[2,256,256]{2,1,0:T(8,128)(2,1)S(1)} collective-permute-done((bf16[2,256,256]{2,1,0:T(8,128)(2,1)}, bf16[2,256,256]{2,1,0:T(8,128)(2,1)S(1)}, u32[]{:S(2)}, u32[]{:S(2)}) %collective-permute-start.7) | collective-permute-done | bytes 262176 | tf_op jit(solution)/shard_map/ppermute | solution.py:195
  102.8 3.9 %collective-permute-done.5.last_a = bf16[2,256,256]{2,1,0:T(8,128)(2,1)S(1)} collective-permute-done((bf16[2,256,256]{2,1,0:T(8,128)(2,1)}, bf16[2,256,256]{2,1,0:T(8,128)(2,1)S(1)}, u32[]{:S(2)}, u32[]{:S(2)}) %collective-permute-start.5) | collective-permute-done | bytes 262176 | tf_op jit(solution)/shard_map/ppermute | solution.py:199
  106.7 1.0 shard_map.96
  107.7 3.5 %all-to-all-start.3 = ((bf16[4,256,256]{2,1,0:T(8,128)(2,1)}), bf16[4,256,256]{2,1,0:T(8,128)(2,1)S(1)}, u32[]{:S(2)}, u32[]{:S(2)}) async-start(bf16[4,256,256]{2,1,0:T(8,128)(2,1)} %shard_map.96), calls=%async_computation.3 | async-start | bytes 1048576 | tf_op jit(solution)/shard_map/all_to_all | solution.py:203
  111.2 1.0 fusion.23.slope_r
  112.3 1.1 select_convert_fusion
  113.4 2.3 %fusion.7 = bf16[768,256]{1,0:T(8,128)(2,1)} fusion(bf16[384,256]{1,0:T(8,128)(2,1)} %bitcast.12, s32[768]{0:T(1024)S(1)} %broadcast_add_fusion, bf16[768,256]{1,0:T(8,128)(2,1)S(1)} %copy-done.1, f32[256]{0:T(256)S(1)} %copy-done.2, f32[768]{0:T(1024)S(1)} %rsqrt.11, pred[768]{0:T(1024)(128)(4,1)S(1)} %broadcast_compare_fusion), kind=kOutput, calls=%fused_computation.12 | convolution fusion | flops 152469504 | bytes 990976 | tf_op jit(solution)/shard_map/dot_general | solution.py:249
  115.7 11.4 %all-to-all-done.3.parts = bf16[4,256,256]{2,1,0:T(8,128)(2,1)S(1)} async-done(((bf16[4,256,256]{2,1,0:T(8,128)(2,1)}), bf16[4,256,256]{2,1,0:T(8,128)(2,1)S(1)}, u32[]{:S(2)}, u32[]{:S(2)}) %all-to-all-start.3) | async-done | bytes 524320 | tf_op jit(solution)/shard_map/all_to_all | solution.py:203
  127.1 0.8 shard_map.97
  (28 shorter events, 2.7 us)
Async XLA Ops:
  0.6 68.7 %collective-permute-start = (bf16[8192,256]{1,0:T(8,128)(2,1)}, bf16[8192,256]{1,0:T(8,128)(2,1)}, u32[]{:S(2)}, u32[]{:S(2)}) collective-permute-start(bf16[8192,256]{1,0:T(8,128)(2,1)} %param.8), channel_id=1, source_target_pairs={{0,1},{1,0},{2,3},{3,2},{4,5},{5,4},{6,7},{7,6},{8,9},{9,8},{10,11... | collective-permute-start | bytes 12582920 | tf_op jit(solution)/shard_map/ppermute | solution.py:191
  6.8 30.3 %all-to-all-start = ((bf16[24,16,256]{2,1,0:T(8,128)(2,1)}), bf16[24,16,256]{2,1,0:T(8,128)(2,1)S(1)}, u32[]{:S(2)}, u32[]{:S(2)}) async-start(bf16[24,16,256]{2,1,0:T(8,128)(2,1)} %bitcast.8), calls=%async_computation | async-start | bytes 393216 | tf_op jit(solution)/shard_map/all_to_all | solution.py:203
  38.1 6.7 %copy-start = (bf16[768,256]{1,0:T(8,128)(2,1)S(1)}, bf16[768,256]{1,0:T(8,128)(2,1)}, u32[]{:S(2)}) copy-start(bf16[768,256]{1,0:T(8,128)(2,1)} %d_r.1) | copy-start | bytes 1179652
  38.2 6.7 %copy-start.1 = (bf16[768,256]{1,0:T(8,128)(2,1)S(1)}, bf16[768,256]{1,0:T(8,128)(2,1)}, u32[]{:S(2)}) copy-start(bf16[768,256]{1,0:T(8,128)(2,1)} %text_r.1) | copy-start | bytes 1179652
  38.2 6.7 %copy-start.2 = (f32[256]{0:T(256)S(1)}, f32[256]{0:T(256)}, u32[]{:S(2)}) copy-start(f32[256]{0:T(256)} %param.12) | copy-start | bytes 3076
  38.2 31.1 %collective-permute-start.3 = (f32[256,256]{1,0:T(8,128)S(1)}, f32[256,256]{1,0:T(8,128)S(1)}, u32[]{:S(2)}, u32[]{:S(2)}) collective-permute-start(f32[256,256]{1,0:T(8,128)S(1)} %fusion.17.image_g.own_g), channel_id=1, source_target_pairs={{0,1},{1,0},{2,3},{3,2},{4,5},{5,4},{6,7},{7,6},{8,9},{9,8},{10,11... | collective-permute-start | bytes 786440 | tf_op jit(solution)/shard_map/ppermute | solution.py:191
  45.9 20.3 %all-to-all-start.1 = ((f32[16,8,256]{2,1,0:T(8,128)}), f32[16,8,256]{2,1,0:T(8,128)S(1)}, u32[]{:S(2)}, u32[]{:S(2)}) async-start(f32[16,8,256]{2,1,0:T(8,128)} %shard_map.94), calls=%async_computation.1 | async-start | bytes 262144 | tf_op jit(solution)/shard_map/all_to_all | solution.py:203
  54.7 13.6 %collective-permute-start.2 = (bf16[256,256]{1,0:T(8,128)(2,1)S(1)}, bf16[256,256]{1,0:T(8,128)(2,1)S(1)}, u32[]{:S(2)}, u32[]{:S(2)}) collective-permute-start(bf16[256,256]{1,0:T(8,128)(2,1)S(1)} %fusion.13.image_r.own_r), channel_id=1, source_target_pairs={{0,1},{1,0},{2,3},{3,2},{4,5},{5,4},{6,7},{7,6},{8,9},{9,8},{10,11... | collective-permute-start | bytes 393224 | tf_op jit(solution)/shard_map/ppermute | solution.py:191
  66.2 3.1 %collective-permute-start.1 = (f32[8,256]{1,0:T(8,128)S(1)}, f32[8,256]{1,0:T(8,128)S(1)}, u32[]{:S(2)}, u32[]{:S(2)}) collective-permute-start(f32[8,256]{1,0:T(8,128)S(1)} %reduce_sum.39.own_s), channel_id=1, source_target_pairs={{0,1},{1,0},{2,3},{3,2},{4,5},{5,4},{6,7},{7,6},{8,9},{9,8},{10,11... | collective-permute-start | bytes 24584 | tf_op jit(solution)/shard_map/ppermute | solution.py:191
  75.3 17.1 %collective-permute-start.6 = (bf16[2,2,256,256]{3,2,1,0:T(8,128)(2,1)S(1)}, bf16[2,2,256,256]{3,2,1,0:T(8,128)(2,1)S(1)}, u32[]{:S(2)}, u32[]{:S(2)}) collective-permute-start(bf16[2,2,256,256]{3,2,1,0:T(8,128)(2,1)S(1)} %get-tuple-element.12), channel_id=1, source_target_pairs={{0,24},{8,16},{16,8},{24,0},{1,25},{9,17},{17,9},{25,1},{2,26},{10... | collective-permute-start | bytes 1572872 | tf_op jit(solution)/shard_map/ppermute | solution.py:199
  78.0 17.0 %collective-permute-start.4 = (bf16[2,2,256,256]{3,2,1,0:T(8,128)(2,1)}, bf16[2,2,256,256]{3,2,1,0:T(8,128)(2,1)S(1)}, u32[]{:S(2)}, u32[]{:S(2)}) collective-permute-start(bf16[2,2,256,256]{3,2,1,0:T(8,128)(2,1)} %get-tuple-element.10), channel_id=1, source_target_pairs={{0,8},{8,0},{16,24},{24,16},{1,9},{9,1},{17,25},{25,17},{2,10},{10... | collective-permute-start | bytes 1572872 | tf_op jit(solution)/shard_map/ppermute | solution.py:195
  80.9 26.9 %all-to-all-start.2 = ((bf16[24,16,256]{2,1,0:T(8,128)(2,1)}), bf16[24,16,256]{2,1,0:T(8,128)(2,1)}, u32[]{:S(2)}, u32[]{:S(2)}) async-start(bf16[24,16,256]{2,1,0:T(8,128)(2,1)} %bitcast.27), calls=%async_computation.2 | async-start | bytes 393216 | tf_op jit(solution)/shard_map/all_to_all | solution.py:203
  93.1 9.7 %collective-permute-start.7 = (bf16[2,256,256]{2,1,0:T(8,128)(2,1)}, bf16[2,256,256]{2,1,0:T(8,128)(2,1)S(1)}, u32[]{:S(2)}, u32[]{:S(2)}) collective-permute-start(bf16[2,256,256]{2,1,0:T(8,128)(2,1)} %fusion.27), channel_id=1, source_target_pairs={{0,8},{8,0},{16,24},{24,16},{1,9},{9,1},{17,25},{25,17},{2,10},{10... | collective-permute-start | bytes 786440 | tf_op jit(solution)/shard_map/ppermute | solution.py:195
  95.8 10.9 %collective-permute-start.5 = (bf16[2,256,256]{2,1,0:T(8,128)(2,1)}, bf16[2,256,256]{2,1,0:T(8,128)(2,1)S(1)}, u32[]{:S(2)}, u32[]{:S(2)}) collective-permute-start(bf16[2,256,256]{2,1,0:T(8,128)(2,1)} %fusion.26), channel_id=1, source_target_pairs={{0,24},{8,16},{16,8},{24,0},{1,25},{9,17},{17,9},{25,1},{2,26},{10... | collective-permute-start | bytes 786440 | tf_op jit(solution)/shard_map/ppermute | solution.py:199
  107.7 19.4 %all-to-all-start.3 = ((bf16[4,256,256]{2,1,0:T(8,128)(2,1)}), bf16[4,256,256]{2,1,0:T(8,128)(2,1)S(1)}, u32[]{:S(2)}, u32[]{:S(2)}) async-start(bf16[4,256,256]{2,1,0:T(8,128)(2,1)} %shard_map.96), calls=%async_computation.3 | async-start | bytes 1048576 | tf_op jit(solution)/shard_map/all_to_all | solution.py:203

commit v3 on v2

v3 whole, which is shorter than its diff:
```python
import jax
import jax.numpy as jnp
from jax import lax
from jax.experimental import pallas as pl
from jax.experimental.pallas import tpu as pltpu
from jax.sharding import Mesh, PartitionSpec as P


TILE = 8
X, Y, C = 4, 4, 2
LANES = 128
GRANT = 16 << 20

epsilon = 1e-05
bf16, f32 = jnp.bfloat16, jnp.float32


def gelu(values):
    return values * (0.5 * (1.0 + lax.erf(values * 0.7071067811865476)))


def gelu_slope(values):
    normal_cdf = 0.5 * (1.0 + lax.erf(values * 0.7071067811865476))
    density = jnp.exp(-0.5 * values * values) * 0.3989422804014327
    return normal_cdf + values * density


def stays(value):
    return pltpu.with_memory_space_constraint(value, pltpu.HBM)


def match_table(wanted, choices_count):
    return wanted[None, :] == jnp.arange(choices_count, dtype=jnp.int32)[:, None]


def outset(tile_pos, group_index, d_normed, groups, capacity):
    tok_dev, cols = d_normed.shape
    total = tile_pos.shape[0]
    spread = tok_dev // TILE
    tiles_dev = total // groups
    slots = groups * capacity

    def kernel(group, pos_r, d_r, given, standing_r, document_r):
        def iota(shape, axis):
            return lax.broadcasted_iota(jnp.int32, shape, axis)

        def one_hot(truth):
            return jnp.where(truth, 1.0, 0.0).astype(bf16)

        def whole_part(values, divisor):
            return jnp.floor((values.astype(f32) + 0.5) * (1.0 / divisor))

        pos = pos_r[...]
        tile = iota((1, total), 1)
        target, source = whole_part(pos, spread), whole_part(tile, tiles_dev)
        pair = target + source * groups
        pair_column = jnp.broadcast_to(pair, (LANES, total)).T[:, :1]
        earlier = (pair_column == pair) & (iota((total, total), 0) < iota((total, total), 1))
        standing = jnp.sum(jnp.where(earlier, 1.0, 0.0), axis=0, keepdims=True).astype(jnp.int32)
        standing_r[...] = standing
        slot = source.astype(jnp.int32) * capacity + standing
        local = pos - group[0] * spread
        arrival = one_hot(iota((LANES, total), 0) == slot)
        place = one_hot(iota((LANES, total), 0) == local)
        tiles = lax.dot_general(
            arrival, place, (((1,), (1,)), ((), ())), preferred_element_type=f32
        ).astype(bf16)
        wide = (slots * TILE, LANES)
        long = (LANES, tok_dev)
        rise = one_hot((iota(wide, 0) // TILE) == iota(wide, 1))
        run = one_hot((iota(long, 1) // TILE) == iota(long, 0))
        spread_tiles = jnp.dot(rise, tiles, preferred_element_type=f32).astype(bf16)
        rows = jnp.dot(spread_tiles, run, preferred_element_type=f32)
        both = rows.shape
        same = (iota(both, 0) % TILE) == (iota(both, 1) % TILE)
        rows = jnp.where(same, rows, 0.0)
        order = (iota(both, 0) + 1).astype(f32)
        document_r[...] = jnp.sum(rows * order, axis=0, keepdims=True).astype(jnp.int32) - 1
        picked = rows.astype(bf16)
        given[...] = jnp.dot(picked, d_r[...], preferred_element_type=f32).astype(bf16)

    vmem = pl.BlockSpec(memory_space=pltpu.VMEM)
    return pl.pallas_call(
        kernel,
        in_specs=[pl.BlockSpec(memory_space=pltpu.SMEM), vmem, vmem],
        out_specs=[vmem] * 3,
        out_shape=[
            jax.ShapeDtypeStruct((slots * TILE, cols), bf16),
            jax.ShapeDtypeStruct((1, total), jnp.int32),
            jax.ShapeDtypeStruct((1, tok_dev), jnp.int32),
        ],
        compiler_params=pltpu.CompilerParams(vmem_limit_bytes=GRANT),
        cost_estimate=pl.CostEstimate(
            flops=2 * slots * TILE * tok_dev * (cols + LANES),
            bytes_accessed=2 * tok_dev * (cols + slots * TILE),
            transcendentals=0,
        ),
    )(group_index.reshape(1), tile_pos.reshape(1, total), d_normed)


def row_sums(image_rows, image_grad, text_embed, d_normed, norm_gain):
    rows, cols = image_rows.shape
    texts = text_embed.shape[0] // rows
    count = 2 + 2 * texts

    def kernel(image_r, image_g, text_r, d_r, gain_r, o_ref, packed):
        lane = lax.broadcasted_iota(jnp.int32, (rows, LANES), 1)
        table = jnp.zeros((rows, LANES), f32)

        def put(table, index, values):
            return jnp.where(lane == index, jnp.sum(values, axis=1, keepdims=True), table)

        wide = image_r[...].astype(f32)
        packed[0] = image_g[...]
        packed[1] = wide
        table = put(table, 0, wide * wide)
        table = put(table, 1, image_g[...] * wide)
        for i in range(texts):
            text = text_r[pl.ds(i * rows, rows), :].astype(f32)
            grad = d_r[pl.ds(i * rows, rows), :].astype(f32) * gain_r[...]
            table = put(table, 2 + i, text * text)
            table = put(table, 2 + texts + i, grad * text)
        flat = table.T[:count]
        o_ref[...] = jnp.broadcast_to(flat[None], (X * Y * C, count, rows))

    return pl.pallas_call(
        kernel,
        out_shape=[
            jax.ShapeDtypeStruct((X * Y * C, count, rows), f32),
            jax.ShapeDtypeStruct((2, rows, cols), f32),
        ],
        compiler_params=pltpu.CompilerParams(vmem_limit_bytes=GRANT),
        cost_estimate=pl.CostEstimate(
            flops=8 * rows * cols * (texts + 2),
            bytes_accessed=4 * rows * cols * (texts + 2),
            transcendentals=0,
        ),
    )(image_rows, image_grad, text_embed, d_normed, norm_gain)


def products(own_weight, pair_weight, inputs, picks, core, slot_rows=None, width=None):
    features, cols = own_weight.shape[-2:]
    half, groups, each = Y // 2, 2, 2
    rows = inputs[0].shape[1] if slot_rows else inputs[1].shape[0]

    def fetches(pick, weights, blocks, sems):
        copies = []
        for n in range(groups * each):
            from_y = pl.ds(n // each * half, half)
            copies.append(
                [
                    pltpu.make_async_copy(
                        weight.at[pick[n], from_y, pick[groups * each]],
                        blocks.at[m, n],
                        sems.at[m, n],
                    )
                    for m, weight in enumerate(weights)
                ]
            )
        for pair in copies:
            for copy in pair:
                copy.start()
        return copies

    def put(copies, blocks, gradients, outs):
        for n, pair in enumerate(copies):
            total = 0.0
            for m, copy in enumerate(pair):
                copy.wait()
                w = blocks[m, n].reshape(half * features, cols)
                total = total + jnp.dot(w, gradients[m][...], preferred_element_type=f32)
            outs[n // each][n % each] = total.astype(bf16).reshape(half, features, rows)

    def first(pick, own_w, pair_w, sums, own_r, own_g, packed, gain, out_a, out_b, own_d, pair_d, normed, blocks, sems):
        copies = fetches(pick, (own_w, pair_w), blocks, sems)
        total = jnp.sum(sums[...], axis=0)
        full = jnp.concatenate([total, jnp.zeros((LANES - total.shape[0], rows), f32)], axis=0)
        columns = full.T
        inverse = lax.rsqrt(columns[:, 0:1] / width + epsilon)
        cross_mean = columns[:, 1:2] / width

        def gradient(wide, grad):
            d_rows = inverse * (grad - wide * inverse * inverse * cross_mean)
            return d_rows.T.astype(bf16)

        wide = own_r[...].astype(f32)
        own_d[...] = gradient(wide, own_g[...])
        pair_d[...] = gradient(packed[1], packed[0])
        put(copies, blocks, (own_d, pair_d), (out_a, out_b))
        normed[...] = (wide * inverse * gain[...]).astype(bf16)

    def second(pick, own_w, pair_w, own_d, pair_d, normed, slot, out_a, out_b, outgoing, blocks, sems):
        copies = fetches(pick, (own_w, pair_w), blocks, sems)
        sender = lax.broadcasted_iota(jnp.int32, (outgoing.shape[0], rows), 0) == slot[...]
        sender = jnp.where(sender, 1.0, 0.0).astype(bf16)
        outgoing[...] = jnp.dot(sender, normed[...], preferred_element_type=f32).astype(bf16)
        put(copies, blocks, (own_d, pair_d), (out_a, out_b))

    out_shape = [jax.ShapeDtypeStruct((each, half, features, rows), bf16)] * groups
    if slot_rows:
        out_shape += [jax.ShapeDtypeStruct((slot_rows, cols), bf16)]
    else:
        out_shape += [pltpu.HBM((cols, rows), bf16)] * 2
        out_shape += [pltpu.HBM((rows, cols), bf16)]
    vmem, hbm = pl.BlockSpec(memory_space=pltpu.VMEM), pl.BlockSpec(memory_space=pltpu.HBM)
    return pl.pallas_call(
        second if slot_rows else first,
        in_specs=[pl.BlockSpec(memory_space=pltpu.SMEM), hbm, hbm] + [vmem] * len(inputs),
        out_specs=[vmem] * len(out_shape),
        out_shape=out_shape,
        scratch_shapes=[
            pltpu.VMEM((C, groups * each, half, features, cols), bf16),
            pltpu.SemaphoreType.DMA((C, groups * each)),
        ],
        compiler_params=pltpu.CompilerParams(vmem_limit_bytes=GRANT),
        cost_estimate=pl.CostEstimate(
            flops=4 * groups * each * half * features * cols * rows,
            bytes_accessed=2 * groups * each * half * features * (2 * cols + rows),
            transcendentals=rows,
        ),
    )(
        jnp.stack([*picks, core]),
        *(stays(weight) for weight in (own_weight, pair_weight)),
        *(stays(value) if slot_rows else value for value in inputs),
    )


def finished(over_y, slope):
    rows, cols = slope.shape

    def kernel(parts, slope_r, o_ref):
        total = jnp.sum(parts[...].astype(f32), axis=0)
        o_ref[...] = (total.T * slope_r[...]).astype(bf16)

    return pl.pallas_call(
        kernel,
        out_shape=jax.ShapeDtypeStruct((rows, cols), bf16),
        compiler_params=pltpu.CompilerParams(vmem_limit_bytes=GRANT),
        cost_estimate=pl.CostEstimate(
            flops=6 * rows * cols, bytes_accessed=14 * rows * cols, transcendentals=0
        ),
    )(over_y, slope)


def combined(kept_a, got_a, last_a, kept_b, got_b, last_b):
    half, features, rows = last_a.shape

    def kernel(kept_a, got_a, last_a, kept_b, got_b, last_b, o_ref):
        for at, parts in ((0, (kept_a, got_a, last_a)), (half, (kept_b, got_b, last_b))):
            total = sum(part[...].astype(f32) for part in parts)
            o_ref[pl.ds(at, half)] = total.astype(bf16)

    second = pl.BlockSpec((None, half, features, rows), lambda i: (1, 0, 0, 0))
    whole = pl.BlockSpec((half, features, rows), lambda i: (0, 0, 0))
    return pl.pallas_call(
        kernel,
        grid=(1,),
        in_specs=[second, second, whole] * 2,
        out_specs=pl.BlockSpec((2 * half, features, rows), lambda i: (0, 0, 0)),
        out_shape=jax.ShapeDtypeStruct((2 * half, features, rows), bf16),
        compiler_params=pltpu.CompilerParams(vmem_limit_bytes=GRANT),
        cost_estimate=pl.CostEstimate(
            flops=4 * half * features * rows,
            bytes_accessed=16 * half * features * rows,
            transcendentals=0,
        ),
    )(kept_a, got_a, last_a, kept_b, got_b, last_b)


def swap_pair(value):
    return lax.ppermute(value, "core", [(0, 1), (1, 0)])


def swap_even(value):
    return lax.ppermute(value, "x", [(i, i ^ 1) for i in range(X)])


def swap_odd(value):
    return lax.ppermute(value, "x", [(i, 3 - i) for i in range(X)])


def swap_all(value, axis):
    return lax.all_to_all(value, axis, split_axis=0, concat_axis=0, tiled=True)


def on_device(hidden, proj_weight, proj_bias, tile_pos, text_embed, norm_gain, d_normed):
    rows_dev, model_width = hidden.shape
    local_cols = proj_weight.shape[1]
    tok_dev = text_embed.shape[0]
    groups = lax.axis_size("grp")
    group_index = lax.axis_index("grp")
    core = lax.axis_index("core")
    here = lax.axis_index("x")
    lane_index = (here * Y + lax.axis_index("y")) * C + core
    tiles_dev = rows_dev // TILE
    spread = tok_dev // TILE
    total_tiles = tiles_dev * groups
    capacity = max(2, (tiles_dev + groups - 1) // groups)
    slot_rows = groups * capacity * TILE

    fetch_out, standing, doc_slot = outset(tile_pos, group_index, d_normed, groups, capacity)
    tile_index = jnp.arange(total_tiles, dtype=jnp.int32)
    slot = tile_pos // spread * capacity + standing[0]
    receiver = (doc_slot == jnp.arange(slot_rows, dtype=jnp.int32)[:, None]).astype(bf16)
    row = jnp.arange(rows_dev, dtype=jnp.int32)
    own_tile = (tile_index - group_index * tiles_dev)[:, None] == (row // TILE)[None, :]
    found = slot[:, None] * TILE + (row % TILE)[None, :]
    image_slot = jnp.sum(jnp.where(own_tile, found, 0), axis=0)
    sender = match_table(image_slot, slot_rows).astype(bf16)

    def scattered(table, rows):
        return lax.dot_general(table, rows, (((0,), (0,)), ((), ())), preferred_element_type=f32)

    def exchange(rows):
        split = rows.reshape(groups, capacity * TILE, local_cols)
        return swap_all(split, "grp").reshape(slot_rows, local_cols)

    fetch_in = exchange(fetch_out)

    pair_weight = swap_pair(proj_weight)

    activated = gelu(hidden.astype(f32)).astype(bf16)
    image_rows = jnp.dot(activated, proj_weight, preferred_element_type=f32) + proj_bias
    image_rows = image_rows.astype(bf16)

    image_cot = scattered(sender, fetch_in).astype(bf16)
    image_grad = image_cot.astype(f32) * norm_gain

    gain_row = norm_gain.reshape(1, local_cols)
    copies, packed = row_sums(image_rows, image_grad, text_embed, d_normed, gain_row)
    sums = swap_all(copies, ("x", "y", "core"))
    pair_image = swap_pair(packed)

    even, odd = here ^ 1, 3 - here
    shape = (X, Y, C, local_cols, local_cols)
    own_weight, pair_weight = proj_weight.reshape(shape), pair_weight.reshape(shape)
    sent_a, sent_b, own_d, pair_d, image_normed = products(
        own_weight,
        pair_weight,
        (sums, image_rows, image_grad, pair_image, gain_row),
        (3 - even, even, odd ^ 1, odd),
        core,
        width=model_width,
    )
    got_a = swap_even(sent_a)
    got_b = swap_odd(sent_b)

    kept_a, kept_b, outgoing = products(
        own_weight,
        pair_weight,
        (own_d, pair_d, image_normed, image_slot.reshape(1, rows_dev)),
        (odd, here, even, here),
        core,
        slot_rows=slot_rows,
    )

    def both(kept, got, index):
        return kept[index].astype(f32) + got[index].astype(f32)

    last_a = swap_odd(both(kept_a, got_a, 0).astype(bf16))
    last_b = swap_even(both(kept_b, got_b, 0).astype(bf16))
    over_x = combined(kept_a, got_a, last_a, kept_b, got_b, last_b)
    over_y = swap_all(over_x, "y")
    own_hidden = lax.dynamic_slice_in_dim(hidden, lane_index * local_cols, local_cols, 1)
    slope = gelu_slope(own_hidden.astype(f32))
    d_hidden = finished(over_y, slope)

    incoming = exchange(outgoing)
    placed = scattered(receiver, incoming).astype(bf16)

    text_sums = jnp.sum(sums[:, 2:], axis=0)
    text_sq, text_cr = text_sums.reshape(2, tok_dev)
    inverse = lax.rsqrt(text_sq / model_width + epsilon)[:, None]
    cross_mean = (text_cr / model_width)[:, None]
    is_image = (doc_slot >= 0).reshape(tok_dev, 1)
    text_wide = text_embed.astype(f32)
    text_grad = d_normed.astype(f32) * norm_gain
    text_normed = (text_wide * inverse * norm_gain).astype(bf16)
    normed = jnp.where(is_image, placed, text_normed)
    d_text = inverse * (text_grad - text_wide * inverse * inverse * cross_mean)
    d_text = jnp.where(is_image, 0.0, d_text).astype(bf16)
    return (normed, d_text, d_hidden)


def solution(mesh):
    groups = mesh.shape["grp"]
    fine = Mesh(mesh.devices.reshape(groups, X, Y, C), ("grp", "x", "y", "core"))
    tp = ("x", "y", "core")
    in_specs = (
        P("grp", None),
        P(None, tp),
        P(tp),
        P(),
        P("grp", tp),
        P(tp),
        P("grp", tp),
    )
    out_specs = (P("grp", tp), P("grp", tp), P("grp", tp))

    return jax.shard_map(on_device, mesh=fine, in_specs=in_specs, out_specs=out_specs, check_vma=False)
```

time: 129 us -> 121 us (0.938)
  the two profiles are of different devices: /device:TPU:8 before, /device:TPU:16 now
where the time goes in v3:
time: 121 us; the launch traced here: 120 us
  starting transfers between devices  49 us (40%)
  waiting for transfers between devices  41.5 us (34%)
  Pallas kernels  14.8 us (12%)
  matrix products  7.19 us (6%)
  other arithmetic  4.79 us (4%)
  local copies, waits for them, and re-layouts  1.9 us (2%)
    all_to_all x4, starting transfers between devices, swap_all(): return lax.all_to_all(value, axis, split_axis=0, concat_axis=0, tiled=True)  34.9 us
    all_to_all x4, waiting for transfers between devices, swap_all(): return lax.all_to_all(value, axis, split_axis=0, concat_axis=0, tiled=True)  31.6 us
    pallas_call x2, Pallas kernels, products(): pl.pallas_call(second if slot_rows else first, in_specs=[pl.BlockSpec(mem...  8.91 us
    ppermute x2, waiting for transfers between devices, swap_odd(): return lax.ppermute(value, 'x', [(i, 3 - i) for i in range(X)])  7.18 us
    ppermute x2, starting transfers between devices, swap_odd(): return lax.ppermute(value, 'x', [(i, 3 - i) for i in range(X)])  6.39 us
    dot_general x1, matrix products, on_device(): jnp.dot(activated, proj_weight, preferred_element_type=f32) + proj_bias  4.62 us
    ppermute x2, starting transfers between devices, swap_even(): return lax.ppermute(value, 'x', [(i, i ^ 1) for i in range(X)])  3.86 us
    ppermute x2, starting transfers between devices, swap_pair(): return lax.ppermute(value, 'core', [(0, 1), (1, 0)])  3.83 us
  transfers between devices with their start and end apart: 10, of which 6 were waited for; matrix products, arithmetic and copies ran while one was open for 11% of the time, Pallas kernels for 8%

profile of v3, /device:TPU:16, one launch (start us, length us, event | category | flops | bytes accessed | tf_op | source)
XLA Modules:
  0.0 120.1 jit_solution(14571587800365317085)
XLA Ops:
  0.6 1.9 %collective-permute-start = (bf16[8192,256]{1,0:T(8,128)(2,1)}, bf16[8192,256]{1,0:T(8,128)(2,1)}, u32[]{:S(2)}, u32[]{:S(2)}) collective-permute-start(bf16[8192,256]{1,0:T(8,128)(2,1)} %param.8), channel_id=1, source_target_pairs={{0,1},{1,0},{2,3},{3,2},{4,5},{5,4},{6,7},{7,6},{8,9},{9,8},{10,11... | collective-permute-start | bytes 12582920 | tf_op jit(solution)/shard_map/ppermute | solution.py:271
  2.6 0.7 reshape.98.pos_r
  3.3 1.0 copy-done
  4.3 1.9 %shard_map.94 = (bf16[384,256]{1,0:T(8,128)(2,1)}, s32[1,768]{1,0:T(1,128)S(1)}, s32[1,768]{1,0:T(1,128)S(1)}) custom-call(s32[1]{0:T(128)} %bitcast.group, s32[1,768]{1,0:T(1,128)S(1)} %reshape.98.pos_r, bf16[768,256]{1,0:T(8,128)(2,1)S(1)} %copy-done), custom_call_target="tpu_custom_call" | custom-call | flops 226492416 | bytes 983040 | tf_op jit(solution)/shard_map/pallas_call | solution.py:83
  6.2 16.4 %all-to-all-start = ((bf16[24,16,256]{2,1,0:T(8,128)(2,1)}), bf16[24,16,256]{2,1,0:T(8,128)(2,1)S(1)}, u32[]{:S(2)}, u32[]{:S(2)}) async-start(bf16[24,16,256]{2,1,0:T(8,128)(2,1)} %bitcast.9), calls=%async_computation | async-start | bytes 393216 | tf_op jit(solution)/shard_map/all_to_all | solution.py:283
  22.6 0.7 fusion.27
  23.6 4.6 %fusion.10.image_r.own_r = bf16[256,256]{1,0:T(8,128)(2,1)S(1)} fusion(bf16[8192,256]{1,0:T(8,128)(2,1)} %param.8, bf16[256,8192]{1,0:T(8,128)(2,1)} %param.7, f32[256]{0:T(256)} %param.9), kind=kOutput, calls=%fused_computation.11 | convolution fusion | flops 1086455808 | bytes 8520704 | tf_op jit(solution)/shard_map/dot_general | solution.py:323
  28.3 9.1 %all-to-all-done = bf16[24,16,256]{2,1,0:T(8,128)(2,1)S(1)} async-done(((bf16[24,16,256]{2,1,0:T(8,128)(2,1)}), bf16[24,16,256]{2,1,0:T(8,128)(2,1)S(1)}, u32[]{:S(2)}, u32[]{:S(2)}) %all-to-all-start) | async-done | bytes 196640 | tf_op jit(solution)/shard_map/all_to_all | solution.py:283
  37.4 0.3 fusion.14.image_g.own_g
  37.7 1.1 shard_map.95
  38.9 1.9 %collective-permute-start.1 = (f32[2,256,256]{2,1,0:T(8,128)S(1)}, f32[2,256,256]{2,1,0:T(8,128)S(1)}, u32[]{:S(2)}, u32[]{:S(2)}) collective-permute-start(f32[2,256,256]{2,1,0:T(8,128)S(1)} %get-tuple-element.20), channel_id=1, source_target_pairs={{0,1},{1,0},{2,3},{3,2},{4,5},{5,4},{6,7},{7,6},{8,9},{9,8},{10,11... | collective-permute-start | bytes 1572872 | tf_op jit(solution)/shard_map/ppermute | solution.py:271
  40.8 9.3 %all-to-all-start.1 = ((f32[32,8,256]{2,1,0:T(8,128)}), f32[32,8,256]{2,1,0:T(8,128)S(1)}, u32[]{:S(2)}, u32[]{:S(2)}) async-start(f32[32,8,256]{2,1,0:T(8,128)} %get-tuple-element.19), calls=%async_computation.1 | async-start | bytes 524288 | tf_op jit(solution)/shard_map/all_to_all | solution.py:283
  50.2 12.1 %all-to-all-done.1.sums = f32[32,8,256]{2,1,0:T(8,128)S(1)} async-done(((f32[32,8,256]{2,1,0:T(8,128)}), f32[32,8,256]{2,1,0:T(8,128)S(1)}, u32[]{:S(2)}, u32[]{:S(2)}) %all-to-all-start.1) | async-done | bytes 262176 | tf_op jit(solution)/shard_map/all_to_all | solution.py:283
  62.2 4.7 %shard_map.96 = (bf16[2,2,256,256]{3,2,1,0:T(8,128)(2,1)}, bf16[2,2,256,256]{3,2,1,0:T(8,128)(2,1)}, bf16[256,256]{1,0:T(8,128)(2,1)}, bf16[256,256]{1,0:T(8,128)(2,1)}, bf16[256,256]{1,0:T(8,128)(2,1)}) custom-call(s32[5]{0:T(128)S(1)} %stack.35.pick, bf16[4,4,2,256,256]{4,3,2,1,0:T(8,128)(2,1)} %bitcast.24, bf16[4,4,2,256,256]{4,3,2,1,0:T(8,128)(2,1)} %bitcast.6.pair_w, ...), custom_call_target="tpu_custom_call" | custom-call | flops 536870912 | bytes 3145728 | tf_op jit(solution)/shard_map/pallas_call | solution.py:206
  67.0 3.2 %collective-permute-start.4 = (bf16[2,2,256,256]{3,2,1,0:T(8,128)(2,1)}, bf16[2,2,256,256]{3,2,1,0:T(8,128)(2,1)S(1)}, u32[]{:S(2)}, u32[]{:S(2)}) collective-permute-start(bf16[2,2,256,256]{3,2,1,0:T(8,128)(2,1)} %get-tuple-element.28), channel_id=1, source_target_pairs={{0,24},{8,16},{16,8},{24,0},{1,25},{9,17},{17,9},{25,1},{2,26},{10... | collective-permute-start | bytes 1572872 | tf_op jit(solution)/shard_map/ppermute | solution.py:279
  70.2 1.9 %collective-permute-start.2 = (bf16[2,2,256,256]{3,2,1,0:T(8,128)(2,1)}, bf16[2,2,256,256]{3,2,1,0:T(8,128)(2,1)S(1)}, u32[]{:S(2)}, u32[]{:S(2)}) collective-permute-start(bf16[2,2,256,256]{3,2,1,0:T(8,128)(2,1)} %get-tuple-element.26), channel_id=1, source_target_pairs={{0,8},{8,0},{16,24},{24,16},{1,9},{9,1},{17,25},{25,17},{2,10},{10... | collective-permute-start | bytes 1572872 | tf_op jit(solution)/shard_map/ppermute | solution.py:275
  72.2 4.2 %shard_map.97 = (bf16[2,2,256,256]{3,2,1,0:T(8,128)(2,1)S(1)}, bf16[2,2,256,256]{3,2,1,0:T(8,128)(2,1)S(1)}, bf16[384,256]{1,0:T(8,128)(2,1)}) custom-call(s32[5]{0:T(128)S(1)} %stack.32.pick, bf16[4,4,2,256,256]{4,3,2,1,0:T(8,128)(2,1)} %bitcast.25, bf16[4,4,2,256,256]{4,3,2,1,0:T(8,128)(2,1)} %bitcast.6.pair_w, bf16[256,256]{1,0:T(8,128)(2,1)} %get-tuple-element.21.own_d, ...), custom_call_target="tpu_custom_call" | custom-call | flops 536870912 | bytes 3145728 | tf_op jit(solution)/shard_map/pallas_call | solution.py:206
  76.4 4.5 %all-to-all-start.2 = ((bf16[24,16,256]{2,1,0:T(8,128)(2,1)}), bf16[24,16,256]{2,1,0:T(8,128)(2,1)}, u32[]{:S(2)}, u32[]{:S(2)}) async-start(bf16[24,16,256]{2,1,0:T(8,128)(2,1)} %bitcast.13), calls=%async_computation.2 | async-start | bytes 393216 | tf_op jit(solution)/shard_map/all_to_all | solution.py:283
  81.0 3.3 %collective-permute-done.4.got_b = bf16[2,2,256,256]{3,2,1,0:T(8,128)(2,1)S(1)} collective-permute-done((bf16[2,2,256,256]{3,2,1,0:T(8,128)(2,1)}, bf16[2,2,256,256]{3,2,1,0:T(8,128)(2,1)S(1)}, u32[]{:S(2)}, u32[]{:S(2)}) %collective-permute-start.4) | collective-permute-done | bytes 524320 | tf_op jit(solution)/shard_map/ppermute | solution.py:279
  84.2 0.8 fusion.23
  85.0 1.9 %collective-permute-start.5 = (bf16[2,256,256]{2,1,0:T(8,128)(2,1)}, bf16[2,256,256]{2,1,0:T(8,128)(2,1)}, u32[]{:S(2)}, u32[]{:S(2)}) collective-permute-start(bf16[2,256,256]{2,1,0:T(8,128)(2,1)} %fusion.23), channel_id=1, source_target_pairs={{0,8},{8,0},{16,24},{24,16},{1,9},{9,1},{17,25},{25,17},{2,10},{10... | collective-permute-start | bytes 786440 | tf_op jit(solution)/shard_map/ppermute | solution.py:275
  86.9 0.8 fusion.22
  87.7 3.2 %collective-permute-start.3 = (bf16[2,256,256]{2,1,0:T(8,128)(2,1)}, bf16[2,256,256]{2,1,0:T(8,128)(2,1)}, u32[]{:S(2)}, u32[]{:S(2)}) collective-permute-start(bf16[2,256,256]{2,1,0:T(8,128)(2,1)} %fusion.22), channel_id=1, source_target_pairs={{0,24},{8,16},{16,8},{24,0},{1,25},{9,17},{17,9},{25,1},{2,26},{10... | collective-permute-start | bytes 786440 | tf_op jit(solution)/shard_map/ppermute | solution.py:279
  90.9 1.0 fusion.19.slope_r
  92.0 2.7 %collective-permute-done.5.last_b = bf16[2,256,256]{2,1,0:T(8,128)(2,1)} collective-permute-done((bf16[2,256,256]{2,1,0:T(8,128)(2,1)}, bf16[2,256,256]{2,1,0:T(8,128)(2,1)}, u32[]{:S(2)}, u32[]{:S(2)}) %collective-permute-start.5) | collective-permute-done | bytes 262176 | tf_op jit(solution)/shard_map/ppermute | solution.py:275
  94.7 3.9 %collective-permute-done.3.last_a = bf16[2,256,256]{2,1,0:T(8,128)(2,1)} collective-permute-done((bf16[2,256,256]{2,1,0:T(8,128)(2,1)}, bf16[2,256,256]{2,1,0:T(8,128)(2,1)}, u32[]{:S(2)}, u32[]{:S(2)}) %collective-permute-start.3) | collective-permute-done | bytes 262176 | tf_op jit(solution)/shard_map/ppermute | solution.py:279
  98.6 2.0 %shard_map.98 = bf16[4,256,256]{2,1,0:T(8,128)(2,1)} custom-call(bf16[2,2,256,256]{3,2,1,0:T(8,128)(2,1)S(1)} %get-tuple-element.25.kept_a, bf16[2,2,256,256]{3,2,1,0:T(8,128)(2,1)S(1)} %collective-permute-done.2.got_a, bf16[2,256,256]{2,1,0:T(8,128)(2,1)} %collective-permute-done.3.last_a, bf16[2,2,256,256]{3,2,1,0:T(8,128)(2,1)S(1)} %get-tuple-element.27.kept_b, ...), custom_call_target="tpu_custom_call" | custom-call | flops 524288 | bytes 2097152 | tf_op jit(solution)/shard_map/pallas_call | solution.py:255
  100.6 4.8 %all-to-all-start.3 = ((bf16[4,256,256]{2,1,0:T(8,128)(2,1)}), bf16[4,256,256]{2,1,0:T(8,128)(2,1)S(1)}, u32[]{:S(2)}, u32[]{:S(2)}) async-start(bf16[4,256,256]{2,1,0:T(8,128)(2,1)} %shard_map.98), calls=%async_computation.3 | async-start | bytes 1048576 | tf_op jit(solution)/shard_map/all_to_all | solution.py:283
  105.4 1.1 select_convert_fusion
  106.6 2.3 %fusion.6 = bf16[768,256]{1,0:T(8,128)(2,1)} fusion(bf16[384,256]{1,0:T(8,128)(2,1)} %bitcast.14, s32[768]{0:T(1024)S(1)} %reduce.1, bf16[768,256]{1,0:T(8,128)(2,1)S(1)} %copy-done.2, f32[256]{0:T(256)S(1)} %copy-done.3, f32[768]{0:T(1024)S(1)} %rsqrt.11, pred[768]{0:T(1024)(128)(4,1)S(1)} %compare_reduce_fusion), kind=kOutput, calls=%fused_computation.8 | convolution fusion | flops 152469504 | bytes 990976 | tf_op jit(solution)/shard_map/dot_general | solution.py:312
  108.8 10.4 %all-to-all-done.3.parts = bf16[4,256,256]{2,1,0:T(8,128)(2,1)S(1)} async-done(((bf16[4,256,256]{2,1,0:T(8,128)(2,1)}), bf16[4,256,256]{2,1,0:T(8,128)(2,1)S(1)}, u32[]{:S(2)}, u32[]{:S(2)}) %all-to-all-start.3) | async-done | bytes 524320 | tf_op jit(solution)/shard_map/all_to_all | solution.py:283
  119.3 0.8 shard_map.99
  (24 shorter events, 0.6 us)
Async XLA Ops:
  0.6 61.6 %collective-permute-start = (bf16[8192,256]{1,0:T(8,128)(2,1)}, bf16[8192,256]{1,0:T(8,128)(2,1)}, u32[]{:S(2)}, u32[]{:S(2)}) collective-permute-start(bf16[8192,256]{1,0:T(8,128)(2,1)} %param.8), channel_id=1, source_target_pairs={{0,1},{1,0},{2,3},{3,2},{4,5},{5,4},{6,7},{7,6},{8,9},{9,8},{10,11... | collective-permute-start | bytes 12582920 | tf_op jit(solution)/shard_map/ppermute | solution.py:271
  3.3 1.0 copy-start
  6.2 31.2 %all-to-all-start = ((bf16[24,16,256]{2,1,0:T(8,128)(2,1)}), bf16[24,16,256]{2,1,0:T(8,128)(2,1)S(1)}, u32[]{:S(2)}, u32[]{:S(2)}) async-start(bf16[24,16,256]{2,1,0:T(8,128)(2,1)} %bitcast.9), calls=%async_computation | async-start | bytes 393216 | tf_op jit(solution)/shard_map/all_to_all | solution.py:283
  23.6 13.8 %copy-start.4 = (s32[256]{0:T(256)}, s32[256]{0:T(256)S(1)}, u32[]{:S(2)}) copy-start(s32[256]{0:T(256)S(1)} %select_reduce_fusion) | copy-start | bytes 3076
  23.6 13.8 %copy-start.3 = (f32[256]{0:T(256)S(1)}, f32[256]{0:T(256)}, u32[]{:S(2)}) copy-start(f32[256]{0:T(256)} %param.12) | copy-start | bytes 3076
  23.6 14.1 %copy-start.1 = (bf16[768,256]{1,0:T(8,128)(2,1)S(1)}, bf16[768,256]{1,0:T(8,128)(2,1)}, u32[]{:S(2)}) copy-start(bf16[768,256]{1,0:T(8,128)(2,1)} %d_r.3) | copy-start | bytes 1179652
  23.6 14.1 %copy-start.2 = (bf16[768,256]{1,0:T(8,128)(2,1)S(1)}, bf16[768,256]{1,0:T(8,128)(2,1)}, u32[]{:S(2)}) copy-start(bf16[768,256]{1,0:T(8,128)(2,1)} %text_r.1) | copy-start | bytes 1179652
  38.9 23.4 %collective-permute-start.1 = (f32[2,256,256]{2,1,0:T(8,128)S(1)}, f32[2,256,256]{2,1,0:T(8,128)S(1)}, u32[]{:S(2)}, u32[]{:S(2)}) collective-permute-start(f32[2,256,256]{2,1,0:T(8,128)S(1)} %get-tuple-element.20), channel_id=1, source_target_pairs={{0,1},{1,0},{2,3},{3,2},{4,5},{5,4},{6,7},{7,6},{8,9},{9,8},{10,11... | collective-permute-start | bytes 1572872 | tf_op jit(solution)/shard_map/ppermute | solution.py:271
  40.8 21.4 %all-to-all-start.1 = ((f32[32,8,256]{2,1,0:T(8,128)}), f32[32,8,256]{2,1,0:T(8,128)S(1)}, u32[]{:S(2)}, u32[]{:S(2)}) async-start(f32[32,8,256]{2,1,0:T(8,128)} %get-tuple-element.19), calls=%async_computation.1 | async-start | bytes 524288 | tf_op jit(solution)/shard_map/all_to_all | solution.py:283
  67.0 17.2 %collective-permute-start.4 = (bf16[2,2,256,256]{3,2,1,0:T(8,128)(2,1)}, bf16[2,2,256,256]{3,2,1,0:T(8,128)(2,1)S(1)}, u32[]{:S(2)}, u32[]{:S(2)}) collective-permute-start(bf16[2,2,256,256]{3,2,1,0:T(8,128)(2,1)} %get-tuple-element.28), channel_id=1, source_target_pairs={{0,24},{8,16},{16,8},{24,0},{1,25},{9,17},{17,9},{25,1},{2,26},{10... | collective-permute-start | bytes 1572872 | tf_op jit(solution)/shard_map/ppermute | solution.py:279
  70.2 16.7 %collective-permute-start.2 = (bf16[2,2,256,256]{3,2,1,0:T(8,128)(2,1)}, bf16[2,2,256,256]{3,2,1,0:T(8,128)(2,1)S(1)}, u32[]{:S(2)}, u32[]{:S(2)}) collective-permute-start(bf16[2,2,256,256]{3,2,1,0:T(8,128)(2,1)} %get-tuple-element.26), channel_id=1, source_target_pairs={{0,8},{8,0},{16,24},{24,16},{1,9},{9,1},{17,25},{25,17},{2,10},{10... | collective-permute-start | bytes 1572872 | tf_op jit(solution)/shard_map/ppermute | solution.py:275
  76.4 24.2 %all-to-all-start.2 = ((bf16[24,16,256]{2,1,0:T(8,128)(2,1)}), bf16[24,16,256]{2,1,0:T(8,128)(2,1)}, u32[]{:S(2)}, u32[]{:S(2)}) async-start(bf16[24,16,256]{2,1,0:T(8,128)(2,1)} %bitcast.13), calls=%async_computation.2 | async-start | bytes 393216 | tf_op jit(solution)/shard_map/all_to_all | solution.py:283
  85.0 9.7 %collective-permute-start.5 = (bf16[2,256,256]{2,1,0:T(8,128)(2,1)}, bf16[2,256,256]{2,1,0:T(8,128)(2,1)}, u32[]{:S(2)}, u32[]{:S(2)}) collective-permute-start(bf16[2,256,256]{2,1,0:T(8,128)(2,1)} %fusion.23), channel_id=1, source_target_pairs={{0,8},{8,0},{16,24},{24,16},{1,9},{9,1},{17,25},{25,17},{2,10},{10... | collective-permute-start | bytes 786440 | tf_op jit(solution)/shard_map/ppermute | solution.py:275
  87.7 10.9 %collective-permute-start.3 = (bf16[2,256,256]{2,1,0:T(8,128)(2,1)}, bf16[2,256,256]{2,1,0:T(8,128)(2,1)}, u32[]{:S(2)}, u32[]{:S(2)}) collective-permute-start(bf16[2,256,256]{2,1,0:T(8,128)(2,1)} %fusion.22), channel_id=1, source_target_pairs={{0,24},{8,16},{16,8},{24,0},{1,25},{9,17},{17,9},{25,1},{2,26},{10... | collective-permute-start | bytes 786440 | tf_op jit(solution)/shard_map/ppermute | solution.py:279
  100.6 18.7 %all-to-all-start.3 = ((bf16[4,256,256]{2,1,0:T(8,128)(2,1)}), bf16[4,256,256]{2,1,0:T(8,128)(2,1)S(1)}, u32[]{:S(2)}, u32[]{:S(2)}) async-start(bf16[4,256,256]{2,1,0:T(8,128)(2,1)} %shard_map.98), calls=%async_computation.3 | async-start | bytes 1048576 | tf_op jit(solution)/shard_map/all_to_all | solution.py:283

commit v4 on v3

--- a/solution.py
+++ b/solution.py
@@ -40,7 +40,10 @@
     tiles_dev = total // groups
     slots = groups * capacity
 
-    def kernel(group, pos_r, d_r, given, standing_r, document_r):
+    def kernel(group, pos_r, d_r, given, standing_r, document_r, d_rows, sem):
+        copy = pltpu.make_async_copy(d_r, d_rows, sem)
+        copy.start()
+
         def iota(shape, axis):
             return lax.broadcasted_iota(jnp.int32, shape, axis)
 
@@ -77,13 +80,19 @@
         order = (iota(both, 0) + 1).astype(f32)
         document_r[...] = jnp.sum(rows * order, axis=0, keepdims=True).astype(jnp.int32) - 1
         picked = rows.astype(bf16)
-        given[...] = jnp.dot(picked, d_r[...], preferred_element_type=f32).astype(bf16)
+        copy.wait()
+        given[...] = jnp.dot(picked, d_rows[...], preferred_element_type=f32).astype(bf16)
 
     vmem = pl.BlockSpec(memory_space=pltpu.VMEM)
     return pl.pallas_call(
         kernel,
-        in_specs=[pl.BlockSpec(memory_space=pltpu.SMEM), vmem, vmem],
+        in_specs=[
+            pl.BlockSpec(memory_space=pltpu.SMEM),
+            vmem,
+            pl.BlockSpec(memory_space=pltpu.HBM),
+        ],
         out_specs=[vmem] * 3,
+        scratch_shapes=[pltpu.VMEM((tok_dev, cols), bf16), pltpu.SemaphoreType.DMA],
         out_shape=[
             jax.ShapeDtypeStruct((slots * TILE, cols), bf16),
             jax.ShapeDtypeStruct((1, total), jnp.int32),
@@ -95,7 +104,7 @@
             bytes_accessed=2 * tok_dev * (cols + slots * TILE),
             transcendentals=0,
         ),
-    )(group_index.reshape(1), tile_pos.reshape(1, total), d_normed)
+    )(group_index.reshape(1), tile_pos.reshape(1, total), stays(d_normed))
 
 
 def row_sums(image_rows, image_grad, text_embed, d_normed, norm_gain):
@@ -121,12 +130,12 @@
             table = put(table, 2 + i, text * text)
             table = put(table, 2 + texts + i, grad * text)
         flat = table.T[:count]
-        o_ref[...] = jnp.broadcast_to(flat[None], (X * Y * C, count, rows))
+        o_ref[...] = jnp.broadcast_to(flat[None], (X * C, count, rows))
 
     return pl.pallas_call(
         kernel,
         out_shape=[
-            jax.ShapeDtypeStruct((X * Y * C, count, rows), f32),
+            jax.ShapeDtypeStruct((X * C, count, rows), f32),
             jax.ShapeDtypeStruct((2, rows, cols), f32),
         ],
         compiler_params=pltpu.CompilerParams(vmem_limit_bytes=GRANT),
@@ -136,6 +145,22 @@
             transcendentals=0,
         ),
     )(image_rows, image_grad, text_embed, d_normed, norm_gain)
+
+
+def summed(parts, copies):
+    _, count, rows = parts.shape
+
+    def kernel(parts_r, o_ref):
+        o_ref[...] = jnp.broadcast_to(jnp.sum(parts_r[...], axis=0)[None], (copies, count, rows))
+
+    return pl.pallas_call(
+        kernel,
+        out_shape=jax.ShapeDtypeStruct((copies, count, rows), f32),
+        compiler_params=pltpu.CompilerParams(vmem_limit_bytes=GRANT),
+        cost_estimate=pl.CostEstimate(
+            flops=parts.size, bytes_accessed=4 * (parts.size + copies * count * rows), transcendentals=0
+        ),
+    )(parts)
 
 
 def products(own_weight, pair_weight, inputs, picks, core, slot_rows=None, width=None):
@@ -328,7 +353,8 @@
 
     gain_row = norm_gain.reshape(1, local_cols)
     copies, packed = row_sums(image_rows, image_grad, text_embed, d_normed, gain_row)
-    sums = swap_all(copies, ("x", "y", "core"))
+    sums = swap_all(copies, ("x", "core"))
+    sums = swap_all(summed(sums, Y), "y")
     pair_image = swap_pair(packed)
 
     even, odd = here ^ 1, 3 - here

time: 121 us -> 118 us (0.975)
  waiting for transfers between devices: 41.5 us -> 29.6 us
  blocking collectives: 0 us -> 9.82 us
    all_to_all x0 -> x1, blocking collectives: none -> 9.82 us  [swap_all(): return lax.all_to_all(value, axis, split_axis=0, concat_axis=0, tiled=True)]
    all_to_all x4, waiting for transfers between devices: 31.6 us -> 23.3 us  [swap_all(): return lax.all_to_all(value, axis, split_axis=0, concat_axis=0, tiled=True)]
    ppermute x2, waiting for transfers between devices: 2.69 us -> 0.32 us  [swap_even(): return lax.ppermute(value, 'x', [(i, i ^ 1) for i in range(X)])]
    all_to_all x4, starting transfers between devices: 34.9 us -> 33.3 us  [swap_all(): return lax.all_to_all(value, axis, split_axis=0, concat_axis=0, tiled=True)]
where the time goes in v4:
time: 118 us; the launch traced here: 117 us
  starting transfers between devices  48.4 us (41%)
  waiting for transfers between devices  29.6 us (25%)
  Pallas kernels  15.2 us (13%)
  blocking collectives  9.82 us (8%)
  matrix products  7.19 us (6%)
  other arithmetic  4.74 us (4%)
    all_to_all x4, starting transfers between devices, swap_all(): return lax.all_to_all(value, axis, split_axis=0, concat_axis=0, tiled=True)  33.3 us
    all_to_all x4, waiting for transfers between devices, swap_all(): return lax.all_to_all(value, axis, split_axis=0, concat_axis=0, tiled=True)  23.3 us
    all_to_all x1, blocking collectives, swap_all(): return lax.all_to_all(value, axis, split_axis=0, concat_axis=0, tiled=True)  9.82 us
    pallas_call x2, Pallas kernels, products(): pl.pallas_call(second if slot_rows else first, in_specs=[pl.BlockSpec(mem...  8.9 us
    ppermute x2, starting transfers between devices, swap_odd(): return lax.ppermute(value, 'x', [(i, 3 - i) for i in range(X)])  7.04 us
    ppermute x2, waiting for transfers between devices, swap_odd(): return lax.ppermute(value, 'x', [(i, 3 - i) for i in range(X)])  6.03 us
    dot_general x1, matrix products, on_device(): jnp.dot(activated, proj_weight, preferred_element_type=f32) + proj_bias  4.62 us
    ppermute x2, starting transfers between devices, swap_even(): return lax.ppermute(value, 'x', [(i, i ^ 1) for i in range(X)])  4.22 us
  transfers between devices with their start and end apart: 10, of which 6 were waited for; matrix products, arithmetic and copies ran while one was open for 11% of the time, Pallas kernels for 8%

profile of v4, /device:TPU:16, one launch (start us, length us, event | category | flops | bytes accessed | tf_op | source)
XLA Modules:
  0.0 116.8 jit_solution(3091850283217609520)
XLA Ops:
  0.6 1.9 %collective-permute-start = (bf16[8192,256]{1,0:T(8,128)(2,1)}, bf16[8192,256]{1,0:T(8,128)(2,1)}, u32[]{:S(2)}, u32[]{:S(2)}) collective-permute-start(bf16[8192,256]{1,0:T(8,128)(2,1)} %param.8), channel_id=1, source_target_pairs={{0,1},{1,0},{2,3},{3,2},{4,5},{5,4},{6,7},{7,6},{8,9},{9,8},{10,11... | collective-permute-start | bytes 12582920 | tf_op jit(solution)/shard_map/ppermute | solution.py:296
  2.6 0.7 reshape.98.pos_r
  3.3 2.5 %shard_map.94 = (bf16[384,256]{1,0:T(8,128)(2,1)}, s32[1,768]{1,0:T(1,128)S(1)}, s32[1,768]{1,0:T(1,128)S(1)}) custom-call(s32[1]{0:T(128)} %bitcast.group, s32[1,768]{1,0:T(1,128)S(1)} %reshape.98.pos_r, bf16[768,256]{1,0:T(8,128)(2,1)} %d_r.3), custom_call_target="tpu_custom_call" | custom-call | flops 226492416 | bytes 983040 | tf_op jit(solution)/shard_map/pallas_call | solution.py:87
  5.8 16.4 %all-to-all-start = ((bf16[24,16,256]{2,1,0:T(8,128)(2,1)}), bf16[24,16,256]{2,1,0:T(8,128)(2,1)S(1)}, u32[]{:S(2)}, u32[]{:S(2)}) async-start(bf16[24,16,256]{2,1,0:T(8,128)(2,1)} %bitcast.9), calls=%async_computation | async-start | bytes 393216 | tf_op jit(solution)/shard_map/all_to_all | solution.py:308
  22.3 0.7 fusion.27
  23.3 4.6 %fusion.10.image_r.own_r = bf16[256,256]{1,0:T(8,128)(2,1)S(1)} fusion(bf16[8192,256]{1,0:T(8,128)(2,1)} %param.8, bf16[256,8192]{1,0:T(8,128)(2,1)} %param.7, f32[256]{0:T(256)} %param.9), kind=kOutput, calls=%fused_computation.11 | convolution fusion | flops 1086455808 | bytes 8520704 | tf_op jit(solution)/shard_map/dot_general | solution.py:348
  27.9 9.1 %all-to-all-done = bf16[24,16,256]{2,1,0:T(8,128)(2,1)S(1)} async-done(((bf16[24,16,256]{2,1,0:T(8,128)(2,1)}), bf16[24,16,256]{2,1,0:T(8,128)(2,1)S(1)}, u32[]{:S(2)}, u32[]{:S(2)}) %all-to-all-start) | async-done | bytes 196640 | tf_op jit(solution)/shard_map/all_to_all | solution.py:308
  37.4 0.4 shard_map.95
  37.8 1.9 %collective-permute-start.1 = (f32[2,256,256]{2,1,0:T(8,128)S(1)}, f32[2,256,256]{2,1,0:T(8,128)S(1)}, u32[]{:S(2)}, u32[]{:S(2)}) collective-permute-start(f32[2,256,256]{2,1,0:T(8,128)S(1)} %get-tuple-element.20), channel_id=1, source_target_pairs={{0,1},{1,0},{2,3},{3,2},{4,5},{5,4},{6,7},{7,6},{8,9},{9,8},{10,11... | collective-permute-start | bytes 1572872 | tf_op jit(solution)/shard_map/ppermute | solution.py:296
  39.7 9.8 %all_to_all.25.parts_r = f32[8,8,256]{2,1,0:T(8,128)S(1)} all-to-all(f32[8,8,256]{2,1,0:T(8,128)S(1)} %get-tuple-element.19), channel_id=1, replica_groups=mesh['grp'=24,'x'=4,'y'=4,'core'=2] {'x','core'}, dimensions={0} | all-to-all | bytes 131072 | tf_op jit(solution)/shard_map/all_to_all | solution.py:308
  49.5 0.6 shard_map.96
  50.2 6.5 %all-to-all-start.2 = ((f32[4,8,256]{2,1,0:T(8,128)}), f32[4,8,256]{2,1,0:T(8,128)S(1)}, u32[]{:S(2)}, u32[]{:S(2)}) async-start(f32[4,8,256]{2,1,0:T(8,128)} %shard_map.96), calls=%async_computation.2 | async-start | bytes 65536 | tf_op jit(solution)/shard_map/all_to_all | solution.py:308
  56.8 5.4 %all-to-all-done.2.sums = f32[4,8,256]{2,1,0:T(8,128)S(1)} async-done(((f32[4,8,256]{2,1,0:T(8,128)}), f32[4,8,256]{2,1,0:T(8,128)S(1)}, u32[]{:S(2)}, u32[]{:S(2)}) %all-to-all-start.2) | async-done | bytes 32800 | tf_op jit(solution)/shard_map/all_to_all | solution.py:308
  62.2 4.7 %shard_map.97 = (bf16[2,2,256,256]{3,2,1,0:T(8,128)(2,1)}, bf16[2,2,256,256]{3,2,1,0:T(8,128)(2,1)}, bf16[256,256]{1,0:T(8,128)(2,1)}, bf16[256,256]{1,0:T(8,128)(2,1)}, bf16[256,256]{1,0:T(8,128)(2,1)}) custom-call(s32[5]{0:T(128)S(1)} %stack.35.pick, bf16[4,4,2,256,256]{4,3,2,1,0:T(8,128)(2,1)} %bitcast.24, bf16[4,4,2,256,256]{4,3,2,1,0:T(8,128)(2,1)} %bitcast.6.pair_w, ...), custom_call_target="tpu_custom_call" | custom-call | flops 536870912 | bytes 3145728 | tf_op jit(solution)/shard_map/pallas_call | solution.py:231
  66.9 3.1 %collective-permute-start.4 = (bf16[2,2,256,256]{3,2,1,0:T(8,128)(2,1)}, bf16[2,2,256,256]{3,2,1,0:T(8,128)(2,1)S(1)}, u32[]{:S(2)}, u32[]{:S(2)}) collective-permute-start(bf16[2,2,256,256]{3,2,1,0:T(8,128)(2,1)} %get-tuple-element.28), channel_id=1, source_target_pairs={{0,24},{8,16},{16,8},{24,0},{1,25},{9,17},{17,9},{25,1},{2,26},{10... | collective-permute-start | bytes 1572872 | tf_op jit(solution)/shard_map/ppermute | solution.py:304
  70.0 1.9 %collective-permute-start.2 = (bf16[2,2,256,256]{3,2,1,0:T(8,128)(2,1)}, bf16[2,2,256,256]{3,2,1,0:T(8,128)(2,1)S(1)}, u32[]{:S(2)}, u32[]{:S(2)}) collective-permute-start(bf16[2,2,256,256]{3,2,1,0:T(8,128)(2,1)} %get-tuple-element.26), channel_id=1, source_target_pairs={{0,8},{8,0},{16,24},{24,16},{1,9},{9,1},{17,25},{25,17},{2,10},{10... | collective-permute-start | bytes 1572872 | tf_op jit(solution)/shard_map/ppermute | solution.py:300
  72.0 4.2 %shard_map.98 = (bf16[2,2,256,256]{3,2,1,0:T(8,128)(2,1)S(1)}, bf16[2,2,256,256]{3,2,1,0:T(8,128)(2,1)S(1)}, bf16[384,256]{1,0:T(8,128)(2,1)}) custom-call(s32[5]{0:T(128)S(1)} %stack.32.pick, bf16[4,4,2,256,256]{4,3,2,1,0:T(8,128)(2,1)} %bitcast.25, bf16[4,4,2,256,256]{4,3,2,1,0:T(8,128)(2,1)} %bitcast.6.pair_w, bf16[256,256]{1,0:T(8,128)(2,1)} %get-tuple-element.21.own_d, ...), custom_call_target="tpu_custom_call" | custom-call | flops 536870912 | bytes 3145728 | tf_op jit(solution)/shard_map/pallas_call | solution.py:231
  76.2 4.5 %all-to-all-start.3 = ((bf16[24,16,256]{2,1,0:T(8,128)(2,1)}), bf16[24,16,256]{2,1,0:T(8,128)(2,1)}, u32[]{:S(2)}, u32[]{:S(2)}) async-start(bf16[24,16,256]{2,1,0:T(8,128)(2,1)} %bitcast.13), calls=%async_computation.3 | async-start | bytes 393216 | tf_op jit(solution)/shard_map/all_to_all | solution.py:308
  80.7 1.6 %collective-permute-done.4.got_b = bf16[2,2,256,256]{3,2,1,0:T(8,128)(2,1)S(1)} collective-permute-done((bf16[2,2,256,256]{3,2,1,0:T(8,128)(2,1)}, bf16[2,2,256,256]{3,2,1,0:T(8,128)(2,1)S(1)}, u32[]{:S(2)}, u32[]{:S(2)}) %collective-permute-start.4) | collective-permute-done | bytes 524320 | tf_op jit(solution)/shard_map/ppermute | solution.py:304
  82.4 0.8 fusion.23
  83.1 2.3 %collective-permute-start.5 = (bf16[2,256,256]{2,1,0:T(8,128)(2,1)}, bf16[2,256,256]{2,1,0:T(8,128)(2,1)S(1)}, u32[]{:S(2)}, u32[]{:S(2)}) collective-permute-start(bf16[2,256,256]{2,1,0:T(8,128)(2,1)} %fusion.23), channel_id=1, source_target_pairs={{0,8},{8,0},{16,24},{24,16},{1,9},{9,1},{17,25},{25,17},{2,10},{10... | collective-permute-start | bytes 786440 | tf_op jit(solution)/shard_map/ppermute | solution.py:300
  85.5 0.8 fusion.22
  86.2 4.0 %collective-permute-start.3 = (bf16[2,256,256]{2,1,0:T(8,128)(2,1)}, bf16[2,256,256]{2,1,0:T(8,128)(2,1)}, u32[]{:S(2)}, u32[]{:S(2)}) collective-permute-start(bf16[2,256,256]{2,1,0:T(8,128)(2,1)} %fusion.22), channel_id=1, source_target_pairs={{0,24},{8,16},{16,8},{24,0},{1,25},{9,17},{17,9},{25,1},{2,26},{10... | collective-permute-start | bytes 786440 | tf_op jit(solution)/shard_map/ppermute | solution.py:304
  90.3 1.0 fusion.19.slope_r
  91.3 0.3 collective-permute-done.5.last_b
  91.6 4.4 %collective-permute-done.3.last_a = bf16[2,256,256]{2,1,0:T(8,128)(2,1)} collective-permute-done((bf16[2,256,256]{2,1,0:T(8,128)(2,1)}, bf16[2,256,256]{2,1,0:T(8,128)(2,1)}, u32[]{:S(2)}, u32[]{:S(2)}) %collective-permute-start.3) | collective-permute-done | bytes 262176 | tf_op jit(solution)/shard_map/ppermute | solution.py:304
  96.0 1.9 %shard_map.99 = bf16[4,256,256]{2,1,0:T(8,128)(2,1)} custom-call(bf16[2,2,256,256]{3,2,1,0:T(8,128)(2,1)S(1)} %get-tuple-element.25.kept_a, bf16[2,2,256,256]{3,2,1,0:T(8,128)(2,1)S(1)} %collective-permute-done.2.got_a, bf16[2,256,256]{2,1,0:T(8,128)(2,1)} %collective-permute-done.3.last_a, bf16[2,2,256,256]{3,2,1,0:T(8,128)(2,1)S(1)} %get-tuple-element.27.kept_b, ...), custom_call_target="tpu_custom_call" | custom-call | flops 524288 | bytes 2097152 | tf_op jit(solution)/shard_map/pallas_call | solution.py:280
  98.0 5.8 %all-to-all-start.4 = ((bf16[4,256,256]{2,1,0:T(8,128)(2,1)}), bf16[4,256,256]{2,1,0:T(8,128)(2,1)S(1)}, u32[]{:S(2)}, u32[]{:S(2)}) async-start(bf16[4,256,256]{2,1,0:T(8,128)(2,1)} %shard_map.99), calls=%async_computation.4 | async-start | bytes 1048576 | tf_op jit(solution)/shard_map/all_to_all | solution.py:308
  103.8 1.1 select_convert_fusion
  104.9 2.3 %fusion.6 = bf16[768,256]{1,0:T(8,128)(2,1)} fusion(bf16[384,256]{1,0:T(8,128)(2,1)} %bitcast.14, s32[768]{0:T(1024)S(1)} %reduce.1, bf16[768,256]{1,0:T(8,128)(2,1)S(1)} %copy-done.1, f32[256]{0:T(256)S(1)} %copy-done.2, f32[768]{0:T(1024)S(1)} %rsqrt.11, pred[768]{0:T(1024)(128)(4,1)S(1)} %compare_reduce_fusion), kind=kOutput, calls=%fused_computation.8 | convolution fusion | flops 152469504 | bytes 990976 | tf_op jit(solution)/shard_map/dot_general | solution.py:337
  107.2 8.8 %all-to-all-done.4.parts = bf16[4,256,256]{2,1,0:T(8,128)(2,1)S(1)} async-done(((bf16[4,256,256]{2,1,0:T(8,128)(2,1)}), bf16[4,256,256]{2,1,0:T(8,128)(2,1)S(1)}, u32[]{:S(2)}, u32[]{:S(2)}) %all-to-all-start.4) | async-done | bytes 524320 | tf_op jit(solution)/shard_map/all_to_all | solution.py:308
  116.0 0.8 shard_map.100
  (24 shorter events, 0.9 us)
Async XLA Ops:
  0.6 61.6 %collective-permute-start = (bf16[8192,256]{1,0:T(8,128)(2,1)}, bf16[8192,256]{1,0:T(8,128)(2,1)}, u32[]{:S(2)}, u32[]{:S(2)}) collective-permute-start(bf16[8192,256]{1,0:T(8,128)(2,1)} %param.8), channel_id=1, source_target_pairs={{0,1},{1,0},{2,3},{3,2},{4,5},{5,4},{6,7},{7,6},{8,9},{9,8},{10,11... | collective-permute-start | bytes 12582920 | tf_op jit(solution)/shard_map/ppermute | solution.py:296
  5.8 31.2 %all-to-all-start = ((bf16[24,16,256]{2,1,0:T(8,128)(2,1)}), bf16[24,16,256]{2,1,0:T(8,128)(2,1)S(1)}, u32[]{:S(2)}, u32[]{:S(2)}) async-start(bf16[24,16,256]{2,1,0:T(8,128)(2,1)} %bitcast.9), calls=%async_computation | async-start | bytes 393216 | tf_op jit(solution)/shard_map/all_to_all | solution.py:308
  23.2 13.8 %copy-start.3 = (s32[256]{0:T(256)}, s32[256]{0:T(256)S(1)}, u32[]{:S(2)}) copy-start(s32[256]{0:T(256)S(1)} %select_reduce_fusion) | copy-start | bytes 3076
  23.3 13.8 %copy-start.2 = (f32[256]{0:T(256)S(1)}, f32[256]{0:T(256)}, u32[]{:S(2)}) copy-start(f32[256]{0:T(256)} %param.12) | copy-start | bytes 3076
  23.3 14.1 %copy-start = (bf16[768,256]{1,0:T(8,128)(2,1)S(1)}, bf16[768,256]{1,0:T(8,128)(2,1)}, u32[]{:S(2)}) copy-start(bf16[768,256]{1,0:T(8,128)(2,1)} %d_r.3) | copy-start | bytes 1179652
  23.3 14.1 %copy-start.1 = (bf16[768,256]{1,0:T(8,128)(2,1)S(1)}, bf16[768,256]{1,0:T(8,128)(2,1)}, u32[]{:S(2)}) copy-start(bf16[768,256]{1,0:T(8,128)(2,1)} %text_r.1) | copy-start | bytes 1179652
  37.8 24.4 %collective-permute-start.1 = (f32[2,256,256]{2,1,0:T(8,128)S(1)}, f32[2,256,256]{2,1,0:T(8,128)S(1)}, u32[]{:S(2)}, u32[]{:S(2)}) collective-permute-start(f32[2,256,256]{2,1,0:T(8,128)S(1)} %get-tuple-element.20), channel_id=1, source_target_pairs={{0,1},{1,0},{2,3},{3,2},{4,5},{5,4},{6,7},{7,6},{8,9},{9,8},{10,11... | collective-permute-start | bytes 1572872 | tf_op jit(solution)/shard_map/ppermute | solution.py:296
  50.2 12.0 %all-to-all-start.2 = ((f32[4,8,256]{2,1,0:T(8,128)}), f32[4,8,256]{2,1,0:T(8,128)S(1)}, u32[]{:S(2)}, u32[]{:S(2)}) async-start(f32[4,8,256]{2,1,0:T(8,128)} %shard_map.96), calls=%async_computation.2 | async-start | bytes 65536 | tf_op jit(solution)/shard_map/all_to_all | solution.py:308
  66.9 15.4 %collective-permute-start.4 = (bf16[2,2,256,256]{3,2,1,0:T(8,128)(2,1)}, bf16[2,2,256,256]{3,2,1,0:T(8,128)(2,1)S(1)}, u32[]{:S(2)}, u32[]{:S(2)}) collective-permute-start(bf16[2,2,256,256]{3,2,1,0:T(8,128)(2,1)} %get-tuple-element.28), channel_id=1, source_target_pairs={{0,24},{8,16},{16,8},{24,0},{1,25},{9,17},{17,9},{25,1},{2,26},{10... | collective-permute-start | bytes 1572872 | tf_op jit(solution)/shard_map/ppermute | solution.py:304
  70.0 15.4 %collective-permute-start.2 = (bf16[2,2,256,256]{3,2,1,0:T(8,128)(2,1)}, bf16[2,2,256,256]{3,2,1,0:T(8,128)(2,1)S(1)}, u32[]{:S(2)}, u32[]{:S(2)}) collective-permute-start(bf16[2,2,256,256]{3,2,1,0:T(8,128)(2,1)} %get-tuple-element.26), channel_id=1, source_target_pairs={{0,8},{8,0},{16,24},{24,16},{1,9},{9,1},{17,25},{25,17},{2,10},{10... | collective-permute-start | bytes 1572872 | tf_op jit(solution)/shard_map/ppermute | solution.py:300
  76.2 21.8 %all-to-all-start.3 = ((bf16[24,16,256]{2,1,0:T(8,128)(2,1)}), bf16[24,16,256]{2,1,0:T(8,128)(2,1)}, u32[]{:S(2)}, u32[]{:S(2)}) async-start(bf16[24,16,256]{2,1,0:T(8,128)(2,1)} %bitcast.13), calls=%async_computation.3 | async-start | bytes 393216 | tf_op jit(solution)/shard_map/all_to_all | solution.py:308
  83.1 8.5 %collective-permute-start.5 = (bf16[2,256,256]{2,1,0:T(8,128)(2,1)}, bf16[2,256,256]{2,1,0:T(8,128)(2,1)S(1)}, u32[]{:S(2)}, u32[]{:S(2)}) collective-permute-start(bf16[2,256,256]{2,1,0:T(8,128)(2,1)} %fusion.23), channel_id=1, source_target_pairs={{0,8},{8,0},{16,24},{24,16},{1,9},{9,1},{17,25},{25,17},{2,10},{10... | collective-permute-start | bytes 786440 | tf_op jit(solution)/shard_map/ppermute | solution.py:300
  86.2 9.8 %collective-permute-start.3 = (bf16[2,256,256]{2,1,0:T(8,128)(2,1)}, bf16[2,256,256]{2,1,0:T(8,128)(2,1)}, u32[]{:S(2)}, u32[]{:S(2)}) collective-permute-start(bf16[2,256,256]{2,1,0:T(8,128)(2,1)} %fusion.22), channel_id=1, source_target_pairs={{0,24},{8,16},{16,8},{24,0},{1,25},{9,17},{17,9},{25,1},{2,26},{10... | collective-permute-start | bytes 786440 | tf_op jit(solution)/shard_map/ppermute | solution.py:304
  98.0 18.0 %all-to-all-start.4 = ((bf16[4,256,256]{2,1,0:T(8,128)(2,1)}), bf16[4,256,256]{2,1,0:T(8,128)(2,1)S(1)}, u32[]{:S(2)}, u32[]{:S(2)}) async-start(bf16[4,256,256]{2,1,0:T(8,128)(2,1)} %shard_map.99), calls=%async_computation.4 | async-start | bytes 1048576 | tf_op jit(solution)/shard_map/all_to_all | solution.py:308

commit v5 on v4

--- a/solution.py
+++ b/solution.py
@@ -187,16 +187,23 @@
                 copy.start()
         return copies
 
-    def put(copies, blocks, gradients, outs):
-        for n, pair in enumerate(copies):
-            total = 0.0
-            for m, copy in enumerate(pair):
-                copy.wait()
-                w = blocks[m, n].reshape(half * features, cols)
-                total = total + jnp.dot(w, gradients[m][...], preferred_element_type=f32)
-            outs[n // each][n % each] = total.astype(bf16).reshape(half, features, rows)
-
-    def first(pick, own_w, pair_w, sums, own_r, own_g, packed, gain, out_a, out_b, own_d, pair_d, normed, blocks, sems):
+    def block_product(copies, blocks, gradients, n):
+        total = 0.0
+        for m, copy in enumerate(copies[n]):
+            copy.wait()
+            w = blocks[m, n].reshape(half * features, cols)
+            total = total + jnp.dot(w, gradients[m][...], preferred_element_type=f32)
+        return total.astype(bf16).reshape(half, features, rows)
+
+    def begun(source, target, sem):
+        copy = pltpu.make_async_copy(source, target, sem)
+        copy.start()
+        return copy
+
+    def first(
+        pick, own_w, pair_w, sums, own_r, own_g, packed, gain, out_a, out_b, own_d, pair_d, normed,
+        blocks, sems, own_v, pair_v, normed_v, out_v, more,
+    ):
         copies = fetches(pick, (own_w, pair_w), blocks, sems)
         total = jnp.sum(sums[...], axis=0)
         full = jnp.concatenate([total, jnp.zeros((LANES - total.shape[0], rows), f32)], axis=0)
@@ -209,33 +216,61 @@
             return d_rows.T.astype(bf16)
 
         wide = own_r[...].astype(f32)
-        own_d[...] = gradient(wide, own_g[...])
-        pair_d[...] = gradient(packed[1], packed[0])
-        put(copies, blocks, (own_d, pair_d), (out_a, out_b))
-        normed[...] = (wide * inverse * gain[...]).astype(bf16)
-
-    def second(pick, own_w, pair_w, own_d, pair_d, normed, slot, out_a, out_b, outgoing, blocks, sems):
+        own_v[...] = gradient(wide, own_g[...])
+        pair_v[...] = gradient(packed[1], packed[0])
+        leaving = [begun(own_v, own_d, more.at[0]), begun(pair_v, pair_d, more.at[1])]
+        for n in range(groups * each):
+            out_v[n] = block_product(copies, blocks, (own_v, pair_v), n)
+            out = (out_a, out_b)[n // each]
+            leaving.append(begun(out_v.at[n], out.at[n % each], more.at[3 + n]))
+        normed_v[...] = (wide * inverse * gain[...]).astype(bf16)
+        leaving.append(begun(normed_v, normed, more.at[2]))
+        for copy in leaving:
+            copy.wait()
+
+    def second(
+        pick, own_w, pair_w, own_d, pair_d, normed, slot, out_a, out_b, outgoing,
+        blocks, sems, own_v, pair_v, normed_v, out_v, more,
+    ):
+        arriving = [begun(own_d, own_v, more.at[0]), begun(pair_d, pair_v, more.at[1])]
+        arriving.append(begun(normed, normed_v, more.at[2]))
         copies = fetches(pick, (own_w, pair_w), blocks, sems)
-        sender = lax.broadcasted_iota(jnp.int32, (outgoing.shape[0], rows), 0) == slot[...]
+        sender = lax.broadcasted_iota(jnp.int32, (slot_rows, rows), 0) == slot[...]
         sender = jnp.where(sender, 1.0, 0.0).astype(bf16)
-        outgoing[...] = jnp.dot(sender, normed[...], preferred_element_type=f32).astype(bf16)
-        put(copies, blocks, (own_d, pair_d), (out_a, out_b))
-
-    out_shape = [jax.ShapeDtypeStruct((each, half, features, rows), bf16)] * groups
+        for copy in arriving:
+            copy.wait()
+        out_v[...] = jnp.dot(sender, normed_v[...], preferred_element_type=f32).astype(bf16)
+        leaving = begun(out_v, outgoing, more.at[3])
+        for n in range(groups * each):
+            out = (out_a, out_b)[n // each]
+            out[n % each] = block_product(copies, blocks, (own_v, pair_v), n)
+        leaving.wait()
+
+    vmem, hbm = pl.BlockSpec(memory_space=pltpu.VMEM), pl.BlockSpec(memory_space=pltpu.HBM)
+    group_shape = (each, half, features, rows)
     if slot_rows:
-        out_shape += [jax.ShapeDtypeStruct((slot_rows, cols), bf16)]
+        out_shape = [jax.ShapeDtypeStruct(group_shape, bf16)] * groups
+        out_shape += [pltpu.HBM((slot_rows, cols), bf16)]
+        in_specs, out_specs = [hbm] * 3 + [vmem], [vmem] * groups + [hbm]
+        held = (slot_rows, cols)
     else:
-        out_shape += [pltpu.HBM((cols, rows), bf16)] * 2
-        out_shape += [pltpu.HBM((rows, cols), bf16)]
-    vmem, hbm = pl.BlockSpec(memory_space=pltpu.VMEM), pl.BlockSpec(memory_space=pltpu.HBM)
+        out_shape = [pltpu.HBM(group_shape, bf16)] * groups
+        out_shape += [pltpu.HBM((cols, rows), bf16)] * 2 + [pltpu.HBM((rows, cols), bf16)]
+        in_specs, out_specs = [vmem] * len(inputs), [hbm] * len(out_shape)
+        held = (groups * each, half, features, rows)
     return pl.pallas_call(
         second if slot_rows else first,
-        in_specs=[pl.BlockSpec(memory_space=pltpu.SMEM), hbm, hbm] + [vmem] * len(inputs),
-        out_specs=[vmem] * len(out_shape),
+        in_specs=[pl.BlockSpec(memory_space=pltpu.SMEM), hbm, hbm] + in_specs,
+        out_specs=out_specs,
         out_shape=out_shape,
         scratch_shapes=[
             pltpu.VMEM((C, groups * each, half, features, cols), bf16),
             pltpu.SemaphoreType.DMA((C, groups * each)),
+            pltpu.VMEM((cols, rows), bf16),
+            pltpu.VMEM((cols, rows), bf16),
+            pltpu.VMEM((rows, cols), bf16),
+            pltpu.VMEM(held, bf16),
+            pltpu.SemaphoreType.DMA((3 + groups * each,)),
         ],
         compiler_params=pltpu.CompilerParams(vmem_limit_bytes=GRANT),
         cost_estimate=pl.CostEstimate(
@@ -246,7 +281,7 @@
     )(
         jnp.stack([*picks, core]),
         *(stays(weight) for weight in (own_weight, pair_weight)),
-        *(stays(value) if slot_rows else value for value in inputs),
+        *(stays(value) if slot_rows and value.dtype == bf16 else value for value in inputs),
     )
 
 

time: 118 us -> 118 us (level)
  no operation moved by 1% of the time
where the time goes in v5:
time: 118 us; the launch traced here: 117 us
  starting transfers between devices  48.4 us (41%)
  waiting for transfers between devices  29.6 us (25%)
  Pallas kernels  15.2 us (13%)
  blocking collectives  9.82 us (8%)
  matrix products  7.19 us (6%)
  other arithmetic  4.74 us (4%)
    all_to_all x4, starting transfers between devices, swap_all(): return lax.all_to_all(value, axis, split_axis=0, concat_axis=0, tiled=True)  33.3 us
    all_to_all x4, waiting for transfers between devices, swap_all(): return lax.all_to_all(value, axis, split_axis=0, concat_axis=0, tiled=True)  23.3 us
    all_to_all x1, blocking collectives, swap_all(): return lax.all_to_all(value, axis, split_axis=0, concat_axis=0, tiled=True)  9.82 us
    pallas_call x2, Pallas kernels, products(): pl.pallas_call(second if slot_rows else first, in_specs=[pl.BlockSpec(mem...  8.85 us
    ppermute x2, starting transfers between devices, swap_odd(): return lax.ppermute(value, 'x', [(i, 3 - i) for i in range(X)])  7.04 us
    ppermute x2, waiting for transfers between devices, swap_odd(): return lax.ppermute(value, 'x', [(i, 3 - i) for i in range(X)])  6.03 us
    dot_general x1, matrix products, on_device(): jnp.dot(activated, proj_weight, preferred_element_type=f32) + proj_bias  4.62 us
    ppermute x2, starting transfers between devices, swap_even(): return lax.ppermute(value, 'x', [(i, i ^ 1) for i in range(X)])  4.25 us
  transfers between devices with their start and end apart: 10, of which 6 were waited for; matrix products, arithmetic and copies ran while one was open for 11% of the time, Pallas kernels for 8%

profile of v5, /device:TPU:16, one launch (start us, length us, event | category | flops | bytes accessed | tf_op | source)
XLA Modules:
  0.0 116.7 jit_solution(13689904193730542410)
XLA Ops:
  0.6 1.9 %collective-permute-start = (bf16[8192,256]{1,0:T(8,128)(2,1)}, bf16[8192,256]{1,0:T(8,128)(2,1)}, u32[]{:S(2)}, u32[]{:S(2)}) collective-permute-start(bf16[8192,256]{1,0:T(8,128)(2,1)} %param.8), channel_id=1, source_target_pairs={{0,1},{1,0},{2,3},{3,2},{4,5},{5,4},{6,7},{7,6},{8,9},{9,8},{10,11... | collective-permute-start | bytes 12582920 | tf_op jit(solution)/shard_map/ppermute | solution.py:331
  2.6 0.7 reshape.98.pos_r
  3.3 2.5 %shard_map.94 = (bf16[384,256]{1,0:T(8,128)(2,1)}, s32[1,768]{1,0:T(1,128)S(1)}, s32[1,768]{1,0:T(1,128)S(1)}) custom-call(s32[1]{0:T(128)} %bitcast.group, s32[1,768]{1,0:T(1,128)S(1)} %reshape.98.pos_r, bf16[768,256]{1,0:T(8,128)(2,1)} %d_r.3), custom_call_target="tpu_custom_call" | custom-call | flops 226492416 | bytes 983040 | tf_op jit(solution)/shard_map/pallas_call | solution.py:87
  5.8 16.4 %all-to-all-start = ((bf16[24,16,256]{2,1,0:T(8,128)(2,1)}), bf16[24,16,256]{2,1,0:T(8,128)(2,1)S(1)}, u32[]{:S(2)}, u32[]{:S(2)}) async-start(bf16[24,16,256]{2,1,0:T(8,128)(2,1)} %bitcast.9), calls=%async_computation | async-start | bytes 393216 | tf_op jit(solution)/shard_map/all_to_all | solution.py:343
  22.3 0.7 fusion.27
  23.3 4.6 %fusion.10.image_r.own_r = bf16[256,256]{1,0:T(8,128)(2,1)S(1)} fusion(bf16[8192,256]{1,0:T(8,128)(2,1)} %param.8, bf16[256,8192]{1,0:T(8,128)(2,1)} %param.7, f32[256]{0:T(256)} %param.9), kind=kOutput, calls=%fused_computation.11 | convolution fusion | flops 1086455808 | bytes 8520704 | tf_op jit(solution)/shard_map/dot_general | solution.py:383
  27.9 9.1 %all-to-all-done = bf16[24,16,256]{2,1,0:T(8,128)(2,1)S(1)} async-done(((bf16[24,16,256]{2,1,0:T(8,128)(2,1)}), bf16[24,16,256]{2,1,0:T(8,128)(2,1)S(1)}, u32[]{:S(2)}, u32[]{:S(2)}) %all-to-all-start) | async-done | bytes 196640 | tf_op jit(solution)/shard_map/all_to_all | solution.py:343
  37.4 0.4 shard_map.95
  37.8 1.9 %collective-permute-start.1 = (f32[2,256,256]{2,1,0:T(8,128)S(1)}, f32[2,256,256]{2,1,0:T(8,128)S(1)}, u32[]{:S(2)}, u32[]{:S(2)}) collective-permute-start(f32[2,256,256]{2,1,0:T(8,128)S(1)} %get-tuple-element.20), channel_id=1, source_target_pairs={{0,1},{1,0},{2,3},{3,2},{4,5},{5,4},{6,7},{7,6},{8,9},{9,8},{10,11... | collective-permute-start | bytes 1572872 | tf_op jit(solution)/shard_map/ppermute | solution.py:331
  39.7 9.8 %all_to_all.25.parts_r = f32[8,8,256]{2,1,0:T(8,128)S(1)} all-to-all(f32[8,8,256]{2,1,0:T(8,128)S(1)} %get-tuple-element.19), channel_id=1, replica_groups=mesh['grp'=24,'x'=4,'y'=4,'core'=2] {'x','core'}, dimensions={0} | all-to-all | bytes 131072 | tf_op jit(solution)/shard_map/all_to_all | solution.py:343
  49.5 0.6 shard_map.96
  50.2 6.5 %all-to-all-start.2 = ((f32[4,8,256]{2,1,0:T(8,128)}), f32[4,8,256]{2,1,0:T(8,128)S(1)}, u32[]{:S(2)}, u32[]{:S(2)}) async-start(f32[4,8,256]{2,1,0:T(8,128)} %shard_map.96), calls=%async_computation.2 | async-start | bytes 65536 | tf_op jit(solution)/shard_map/all_to_all | solution.py:343
  56.8 5.4 %all-to-all-done.2.sums = f32[4,8,256]{2,1,0:T(8,128)S(1)} async-done(((f32[4,8,256]{2,1,0:T(8,128)}), f32[4,8,256]{2,1,0:T(8,128)S(1)}, u32[]{:S(2)}, u32[]{:S(2)}) %all-to-all-start.2) | async-done | bytes 32800 | tf_op jit(solution)/shard_map/all_to_all | solution.py:343
  62.2 4.6 %shard_map.97 = (bf16[2,2,256,256]{3,2,1,0:T(8,128)(2,1)}, bf16[2,2,256,256]{3,2,1,0:T(8,128)(2,1)}, bf16[256,256]{1,0:T(8,128)(2,1)}, bf16[256,256]{1,0:T(8,128)(2,1)}, bf16[256,256]{1,0:T(8,128)(2,1)}) custom-call(s32[5]{0:T(128)S(1)} %stack.35.pick, bf16[4,4,2,256,256]{4,3,2,1,0:T(8,128)(2,1)} %bitcast.25, bf16[4,4,2,256,256]{4,3,2,1,0:T(8,128)(2,1)} %bitcast.6.pair_w, ...), custom_call_target="tpu_custom_call" | custom-call | flops 536870912 | bytes 3145728 | tf_op jit(solution)/shard_map/pallas_call | solution.py:261
  66.8 3.1 %collective-permute-start.4 = (bf16[2,2,256,256]{3,2,1,0:T(8,128)(2,1)}, bf16[2,2,256,256]{3,2,1,0:T(8,128)(2,1)S(1)}, u32[]{:S(2)}, u32[]{:S(2)}) collective-permute-start(bf16[2,2,256,256]{3,2,1,0:T(8,128)(2,1)} %get-tuple-element.28), channel_id=1, source_target_pairs={{0,24},{8,16},{16,8},{24,0},{1,25},{9,17},{17,9},{25,1},{2,26},{10... | collective-permute-start | bytes 1572872 | tf_op jit(solution)/shard_map/ppermute | solution.py:339
  69.9 1.9 %collective-permute-start.2 = (bf16[2,2,256,256]{3,2,1,0:T(8,128)(2,1)}, bf16[2,2,256,256]{3,2,1,0:T(8,128)(2,1)S(1)}, u32[]{:S(2)}, u32[]{:S(2)}) collective-permute-start(bf16[2,2,256,256]{3,2,1,0:T(8,128)(2,1)} %get-tuple-element.26), channel_id=1, source_target_pairs={{0,8},{8,0},{16,24},{24,16},{1,9},{9,1},{17,25},{25,17},{2,10},{10... | collective-permute-start | bytes 1572872 | tf_op jit(solution)/shard_map/ppermute | solution.py:335
  71.9 4.2 %shard_map.98 = (bf16[2,2,256,256]{3,2,1,0:T(8,128)(2,1)S(1)}, bf16[2,2,256,256]{3,2,1,0:T(8,128)(2,1)S(1)}, bf16[384,256]{1,0:T(8,128)(2,1)}) custom-call(s32[5]{0:T(128)S(1)} %stack.32.pick, bf16[4,4,2,256,256]{4,3,2,1,0:T(8,128)(2,1)} %bitcast.26, bf16[4,4,2,256,256]{4,3,2,1,0:T(8,128)(2,1)} %bitcast.6.pair_w, bf16[256,256]{1,0:T(8,128)(2,1)} %get-tuple-element.21.own_d, ...), custom_call_target="tpu_custom_call" | custom-call | flops 536870912 | bytes 3145728 | tf_op jit(solution)/shard_map/pallas_call | solution.py:261
  76.2 4.5 %all-to-all-start.3 = ((bf16[24,16,256]{2,1,0:T(8,128)(2,1)}), bf16[24,16,256]{2,1,0:T(8,128)(2,1)}, u32[]{:S(2)}, u32[]{:S(2)}) async-start(bf16[24,16,256]{2,1,0:T(8,128)(2,1)} %bitcast.28), calls=%async_computation.3 | async-start | bytes 393216 | tf_op jit(solution)/shard_map/all_to_all | solution.py:343
  80.7 1.6 %collective-permute-done.4.got_b = bf16[2,2,256,256]{3,2,1,0:T(8,128)(2,1)S(1)} collective-permute-done((bf16[2,2,256,256]{3,2,1,0:T(8,128)(2,1)}, bf16[2,2,256,256]{3,2,1,0:T(8,128)(2,1)S(1)}, u32[]{:S(2)}, u32[]{:S(2)}) %collective-permute-start.4) | collective-permute-done | bytes 524320 | tf_op jit(solution)/shard_map/ppermute | solution.py:339
  82.3 0.8 fusion.23
  83.1 2.3 %collective-permute-start.5 = (bf16[2,256,256]{2,1,0:T(8,128)(2,1)}, bf16[2,256,256]{2,1,0:T(8,128)(2,1)S(1)}, u32[]{:S(2)}, u32[]{:S(2)}) collective-permute-start(bf16[2,256,256]{2,1,0:T(8,128)(2,1)} %fusion.23), channel_id=1, source_target_pairs={{0,8},{8,0},{16,24},{24,16},{1,9},{9,1},{17,25},{25,17},{2,10},{10... | collective-permute-start | bytes 786440 | tf_op jit(solution)/shard_map/ppermute | solution.py:335
  85.4 0.8 fusion.22
  86.2 4.0 %collective-permute-start.3 = (bf16[2,256,256]{2,1,0:T(8,128)(2,1)}, bf16[2,256,256]{2,1,0:T(8,128)(2,1)}, u32[]{:S(2)}, u32[]{:S(2)}) collective-permute-start(bf16[2,256,256]{2,1,0:T(8,128)(2,1)} %fusion.22), channel_id=1, source_target_pairs={{0,24},{8,16},{16,8},{24,0},{1,25},{9,17},{17,9},{25,1},{2,26},{10... | collective-permute-start | bytes 786440 | tf_op jit(solution)/shard_map/ppermute | solution.py:339
  90.2 1.0 fusion.19.slope_r
  91.2 0.3 collective-permute-done.5.last_b
  91.5 4.4 %collective-permute-done.3.last_a = bf16[2,256,256]{2,1,0:T(8,128)(2,1)} collective-permute-done((bf16[2,256,256]{2,1,0:T(8,128)(2,1)}, bf16[2,256,256]{2,1,0:T(8,128)(2,1)}, u32[]{:S(2)}, u32[]{:S(2)}) %collective-permute-start.3) | collective-permute-done | bytes 262176 | tf_op jit(solution)/shard_map/ppermute | solution.py:339
  96.0 2.0 %shard_map.99 = bf16[4,256,256]{2,1,0:T(8,128)(2,1)} custom-call(bf16[2,2,256,256]{3,2,1,0:T(8,128)(2,1)S(1)} %get-tuple-element.25.kept_a, bf16[2,2,256,256]{3,2,1,0:T(8,128)(2,1)S(1)} %collective-permute-done.2.got_a, bf16[2,256,256]{2,1,0:T(8,128)(2,1)} %collective-permute-done.3.last_a, bf16[2,2,256,256]{3,2,1,0:T(8,128)(2,1)S(1)} %get-tuple-element.27.kept_b, ...), custom_call_target="tpu_custom_call" | custom-call | flops 524288 | bytes 2097152 | tf_op jit(solution)/shard_map/pallas_call | solution.py:315
  97.9 5.8 %all-to-all-start.4 = ((bf16[4,256,256]{2,1,0:T(8,128)(2,1)}), bf16[4,256,256]{2,1,0:T(8,128)(2,1)S(1)}, u32[]{:S(2)}, u32[]{:S(2)}) async-start(bf16[4,256,256]{2,1,0:T(8,128)(2,1)} %shard_map.99), calls=%async_computation.4 | async-start | bytes 1048576 | tf_op jit(solution)/shard_map/all_to_all | solution.py:343
  103.8 1.1 select_convert_fusion
  104.9 2.3 %fusion.6 = bf16[768,256]{1,0:T(8,128)(2,1)} fusion(bf16[384,256]{1,0:T(8,128)(2,1)} %bitcast.14, s32[768]{0:T(1024)S(1)} %reduce.1, bf16[768,256]{1,0:T(8,128)(2,1)S(1)} %copy-done.1, f32[256]{0:T(256)S(1)} %copy-done.2, f32[768]{0:T(1024)S(1)} %rsqrt.11, pred[768]{0:T(1024)(128)(4,1)S(1)} %compare_reduce_fusion), kind=kOutput, calls=%fused_computation.8 | convolution fusion | flops 152469504 | bytes 990976 | tf_op jit(solution)/shard_map/dot_general | solution.py:372
  107.2 8.7 %all-to-all-done.4.parts = bf16[4,256,256]{2,1,0:T(8,128)(2,1)S(1)} async-done(((bf16[4,256,256]{2,1,0:T(8,128)(2,1)}), bf16[4,256,256]{2,1,0:T(8,128)(2,1)S(1)}, u32[]{:S(2)}, u32[]{:S(2)}) %all-to-all-start.4) | async-done | bytes 524320 | tf_op jit(solution)/shard_map/all_to_all | solution.py:343
  115.9 0.8 shard_map.100
  (22 shorter events, 0.9 us)
Async XLA Ops:
  0.6 61.6 %collective-permute-start = (bf16[8192,256]{1,0:T(8,128)(2,1)}, bf16[8192,256]{1,0:T(8,128)(2,1)}, u32[]{:S(2)}, u32[]{:S(2)}) collective-permute-start(bf16[8192,256]{1,0:T(8,128)(2,1)} %param.8), channel_id=1, source_target_pairs={{0,1},{1,0},{2,3},{3,2},{4,5},{5,4},{6,7},{7,6},{8,9},{9,8},{10,11... | collective-permute-start | bytes 12582920 | tf_op jit(solution)/shard_map/ppermute | solution.py:331
  5.8 31.2 %all-to-all-start = ((bf16[24,16,256]{2,1,0:T(8,128)(2,1)}), bf16[24,16,256]{2,1,0:T(8,128)(2,1)S(1)}, u32[]{:S(2)}, u32[]{:S(2)}) async-start(bf16[24,16,256]{2,1,0:T(8,128)(2,1)} %bitcast.9), calls=%async_computation | async-start | bytes 393216 | tf_op jit(solution)/shard_map/all_to_all | solution.py:343
  23.2 13.8 %copy-start.2 = (f32[256]{0:T(256)S(1)}, f32[256]{0:T(256)}, u32[]{:S(2)}) copy-start(f32[256]{0:T(256)} %param.12) | copy-start | bytes 3076
  23.3 14.1 %copy-start = (bf16[768,256]{1,0:T(8,128)(2,1)S(1)}, bf16[768,256]{1,0:T(8,128)(2,1)}, u32[]{:S(2)}) copy-start(bf16[768,256]{1,0:T(8,128)(2,1)} %d_r.3) | copy-start | bytes 1179652
  23.3 14.1 %copy-start.1 = (bf16[768,256]{1,0:T(8,128)(2,1)S(1)}, bf16[768,256]{1,0:T(8,128)(2,1)}, u32[]{:S(2)}) copy-start(bf16[768,256]{1,0:T(8,128)(2,1)} %text_r.1) | copy-start | bytes 1179652
  37.8 24.4 %collective-permute-start.1 = (f32[2,256,256]{2,1,0:T(8,128)S(1)}, f32[2,256,256]{2,1,0:T(8,128)S(1)}, u32[]{:S(2)}, u32[]{:S(2)}) collective-permute-start(f32[2,256,256]{2,1,0:T(8,128)S(1)} %get-tuple-element.20), channel_id=1, source_target_pairs={{0,1},{1,0},{2,3},{3,2},{4,5},{5,4},{6,7},{7,6},{8,9},{9,8},{10,11... | collective-permute-start | bytes 1572872 | tf_op jit(solution)/shard_map/ppermute | solution.py:331
  50.2 12.0 %all-to-all-start.2 = ((f32[4,8,256]{2,1,0:T(8,128)}), f32[4,8,256]{2,1,0:T(8,128)S(1)}, u32[]{:S(2)}, u32[]{:S(2)}) async-start(f32[4,8,256]{2,1,0:T(8,128)} %shard_map.96), calls=%async_computation.2 | async-start | bytes 65536 | tf_op jit(solution)/shard_map/all_to_all | solution.py:343
  66.8 15.4 %collective-permute-start.4 = (bf16[2,2,256,256]{3,2,1,0:T(8,128)(2,1)}, bf16[2,2,256,256]{3,2,1,0:T(8,128)(2,1)S(1)}, u32[]{:S(2)}, u32[]{:S(2)}) collective-permute-start(bf16[2,2,256,256]{3,2,1,0:T(8,128)(2,1)} %get-tuple-element.28), channel_id=1, source_target_pairs={{0,24},{8,16},{16,8},{24,0},{1,25},{9,17},{17,9},{25,1},{2,26},{10... | collective-permute-start | bytes 1572872 | tf_op jit(solution)/shard_map/ppermute | solution.py:339
  69.9 15.5 %collective-permute-start.2 = (bf16[2,2,256,256]{3,2,1,0:T(8,128)(2,1)}, bf16[2,2,256,256]{3,2,1,0:T(8,128)(2,1)S(1)}, u32[]{:S(2)}, u32[]{:S(2)}) collective-permute-start(bf16[2,2,256,256]{3,2,1,0:T(8,128)(2,1)} %get-tuple-element.26), channel_id=1, source_target_pairs={{0,8},{8,0},{16,24},{24,16},{1,9},{9,1},{17,25},{25,17},{2,10},{10... | collective-permute-start | bytes 1572872 | tf_op jit(solution)/shard_map/ppermute | solution.py:335
  76.2 21.8 %all-to-all-start.3 = ((bf16[24,16,256]{2,1,0:T(8,128)(2,1)}), bf16[24,16,256]{2,1,0:T(8,128)(2,1)}, u32[]{:S(2)}, u32[]{:S(2)}) async-start(bf16[24,16,256]{2,1,0:T(8,128)(2,1)} %bitcast.28), calls=%async_computation.3 | async-start | bytes 393216 | tf_op jit(solution)/shard_map/all_to_all | solution.py:343
  83.1 8.5 %collective-permute-start.5 = (bf16[2,256,256]{2,1,0:T(8,128)(2,1)}, bf16[2,256,256]{2,1,0:T(8,128)(2,1)S(1)}, u32[]{:S(2)}, u32[]{:S(2)}) collective-permute-start(bf16[2,256,256]{2,1,0:T(8,128)(2,1)} %fusion.23), channel_id=1, source_target_pairs={{0,8},{8,0},{16,24},{24,16},{1,9},{9,1},{17,25},{25,17},{2,10},{10... | collective-permute-start | bytes 786440 | tf_op jit(solution)/shard_map/ppermute | solution.py:335
  86.2 9.8 %collective-permute-start.3 = (bf16[2,256,256]{2,1,0:T(8,128)(2,1)}, bf16[2,256,256]{2,1,0:T(8,128)(2,1)}, u32[]{:S(2)}, u32[]{:S(2)}) collective-permute-start(bf16[2,256,256]{2,1,0:T(8,128)(2,1)} %fusion.22), channel_id=1, source_target_pairs={{0,24},{8,16},{16,8},{24,0},{1,25},{9,17},{17,9},{25,1},{2,26},{10... | collective-permute-start | bytes 786440 | tf_op jit(solution)/shard_map/ppermute | solution.py:339
  97.9 18.0 %all-to-all-start.4 = ((bf16[4,256,256]{2,1,0:T(8,128)(2,1)}), bf16[4,256,256]{2,1,0:T(8,128)(2,1)S(1)}, u32[]{:S(2)}, u32[]{:S(2)}) async-start(bf16[4,256,256]{2,1,0:T(8,128)(2,1)} %shard_map.99), calls=%async_computation.4 | async-start | bytes 1048576 | tf_op jit(solution)/shard_map/all_to_all | solution.py:343
